TPU v7x, 256 devices: a 8x8x2 block of a 8x8x16 slice. The times are simulated.
256 devices in a mesh: rep: 2 (over z), kv: 128 (over x, y, core).
Axes of the slice: x: 8, y: 8, z: 2, core: 2. Of those that a mesh axis runs over, the one named last changes fastest.
The devices are a block of a 8x8x16 slice.
Arguments:
- queries: bfloat16 [32, 3, 36864], P('rep', None, 'kv'), parts along dimension 0, may hold values from -4 to 4
- cache: bfloat16 [65536, 16, 576], P(('rep', 'kv')), parts along dimension 0, may hold values from -4 to 4
- page_counts: int32 [32], P('rep'), parts along dimension 0, may hold values from 1 to 16384, as said below
- slot_request: int32 [8192], P(('rep', 'kv')), parts along dimension 0, may hold values from 0 to 15, as said below
- slot_start: int32 [8192], P(('rep', 'kv')), parts along dimension 0, may hold values from 0 to 16376, as said below
- slot_live: int32 [8192], P(('rep', 'kv')), parts along dimension 0, may hold values from 1 to 8, as said below
- slot_pages: int32 [8192, 8], P(('rep', 'kv')), parts along dimension 0, may hold values from 0 to 255, as said below
Outputs:
- attended: bfloat16 [32, 3, 32768], P('rep', None, 'kv'), parts along dimension 0
- lse: float32 [32, 3, 64], P('rep'), parts along dimension 0
There are 2 independent parts, one for each index of `rep`. A program takes and returns all parts, laid end to end along the dimension named above; each array names one. Nothing has to cross between parts.
Inputs may be any that keep to these rules, and one draw needn't show every extreme that they name: Request r has 16 * page_counts[r] tokens; the slots that name r cover its pages 0 to page_counts[r] - 1, each exactly once; one request holds 8 * (2048) pages. `slot_request`: every request is named by at least one slot; slot s lives on index s // 32 of kv. Slot s covers pages slot_start[s] to slot_start[s] + slot_live[s] - 1 of its request. Only the first slot_live[s] entries of slot_pages[s] are used. `slot_pages`: page numbers local to the device that holds the slot; all entries of one device's slots are distinct.
All inputs are finite; a program needn't handle non-finite values.
Results may differ from a plain program's by a relative error of at most 0.0043.
Values may be sent and summed in bfloat16 or wider, within the bound.
A program may use at most 128 MiB of HBM per device.

v0:
```python
import jax
import jax.numpy as jnp
from jax import lax
from jax.sharding import Mesh
from jax.sharding import PartitionSpec as P

ROPE = 64
KV = ("kv_0", "kv_1", "kv_2")
REP_KV = ("rep", "kv_0", "kv_1", "kv_2")


softmax_scale = 192.0 ** (-0.5)
neg_floor = -1e30
block_slots = 8


def in_order(blocks, dim):
    dims = list(blocks.shape[1:])
    dims[dim] *= blocks.shape[0]
    return jnp.moveaxis(blocks, 0, dim).reshape(dims)


def gather_in_order(array, axes, turns):
    blocks = array[None]
    for k in turns:
        blocks = lax.all_gather(blocks, axes[k], axis=0, tiled=True)
    current = [lax.axis_size(axes[k]) for k in reversed(turns)]
    blocks = blocks.reshape(*current, *array.shape)
    turned = sorted(range(len(turns)), key=lambda place: turns[len(turns) - 1 - place])
    return blocks.transpose(*turned, *range(len(turns), blocks.ndim)).reshape(-1, *array.shape)


def gathered_by_axis(array, axes, turns, dim):
    return in_order(gather_in_order(array, axes, turns), dim)


def cut_along(array, dim, count):
    dims = array.shape
    blocks = array.reshape(*dims[:dim], count, dims[dim] // count, *dims[dim + 1 :])
    return jnp.moveaxis(blocks, dim, 0)


def cut_rows(length, count):
    unit = 8 if length >= 8 * count else 1
    return [length // unit * k // count * unit for k in range(1, count)]


def cut_exchange(array, axis, pieces, split_dim, concat_dim):
    blocks = cut_along(array, split_dim, lax.axis_size(axis))
    split_at = max(range(1, max(2, blocks.ndim - 1)), key=lambda d: blocks.shape[d])
    done = []
    for piece in jnp.split(blocks, cut_rows(blocks.shape[split_at], pieces), axis=split_at):
        if piece.size:
            done.append(lax.all_to_all(piece, axis, split_axis=0, concat_axis=0, tiled=True))
    return in_order(jnp.concatenate(done, axis=split_at), concat_dim)


def sent_together(arrays, axis, dim, along):
    ends, at = ([], 0)
    for a in arrays[:-1]:
        at += a.shape[along]
        ends.append(at)
    both = jnp.concatenate(arrays, axis=along)
    return tuple(jnp.split(lax.all_gather(both, axis, axis=dim, tiled=True), ends, axis=along))


def slot_partials(
    query_heads, key_rows, request, first_page, live_pages, page_counts, page_rows, latent
):
    row_count = key_rows.shape[1]
    query_count = query_heads.shape[1]
    request_count = page_counts.shape[0]
    chosen = query_heads[request]
    scores = (
        jnp.einsum("gqhc,gjc->gqhj", chosen, key_rows, preferred_element_type=jnp.float32)
        * softmax_scale
    )
    row_ids = jnp.arange(row_count, dtype=jnp.int32)
    page_of = row_ids // page_rows
    position = (first_page[:, None] + page_of[None, :]) * page_rows + row_ids[None, :] % page_rows
    member = request[:, None] == jnp.arange(request_count, dtype=jnp.int32)[None, :]
    request_pages = jnp.sum(jnp.where(member, page_counts[None, :], 0), axis=1)
    query_ids = jnp.arange(query_count, dtype=jnp.int32)
    limit = request_pages[:, None] * page_rows - (query_count - 1 - query_ids)[None, :]
    visible = (page_of[None, None, :] < live_pages[:, None, None]) & (
        position[:, None, :] < limit[:, :, None]
    )
    visible = visible[:, :, None, :]
    slot_max = jnp.max(jnp.where(visible, scores, neg_floor), axis=3)
    shifted = jnp.where(visible, scores - slot_max[..., None], neg_floor)
    weights = jnp.exp(shifted)
    slot_sum = jnp.sum(weights, axis=3)
    rounded = weights.astype(jnp.bfloat16)
    slot_out = jnp.einsum(
        "gqhj,gjc->gqhc", rounded, key_rows[:, :, :latent], preferred_element_type=jnp.float32
    )
    return (slot_max, slot_sum, slot_out)


def fold_slots(carry, request, slot_max, slot_sum, slot_out):
    best, denom, numer = carry
    request_count = best.shape[0]
    member = request[:, None] == jnp.arange(request_count, dtype=jnp.int32)[None, :]
    block_best = jnp.max(jnp.where(member[:, :, None, None], slot_max[:, None], neg_floor), axis=0)
    new_best = jnp.maximum(best, block_best)
    kept = jnp.exp(best - new_best)
    member_float = member.astype(jnp.float32)
    slot_best = jnp.einsum("gr,rqh->gqh", member_float, new_best, precision=lax.Precision.HIGHEST)
    factor = jnp.exp(slot_max - slot_best)
    denom = denom * kept + jnp.einsum(
        "gr,gqh->rqh", member_float, factor * slot_sum, precision=lax.Precision.HIGHEST
    )
    numer = numer * kept[..., None] + jnp.einsum(
        "gr,gqhc->rqhc", member_float, factor[..., None] * slot_out, precision=lax.Precision.HIGHEST
    )
    return (new_best, denom, numer)


def per_device(queries, cache, page_counts, slot_request, slot_start, slot_live, slot_pages):
    gathered = gathered_by_axis(queries, KV, (0, 1, 2), 2)
    request_count, query_count, flat_width = gathered.shape
    token_width = cache.shape[2]
    head_count = flat_width // token_width
    latent = token_width - ROPE
    page_rows = cache.shape[1]
    query_heads = gathered.reshape(request_count, query_count, head_count, token_width)
    local_slots = slot_request.shape[0]
    slot_span = slot_pages.shape[1]
    block_count = local_slots // block_slots

    def one_block(carry, block_index):
        first_slot = block_index * block_slots

        def pick_rows(source):
            return lax.dynamic_slice_in_dim(source, first_slot, block_slots, 0)

        request = pick_rows(slot_request)
        first_page = pick_rows(slot_start)
        live_pages = pick_rows(slot_live)
        pages = pick_rows(slot_pages)
        key_rows = cache[pages.reshape(-1)].reshape(block_slots, slot_span * page_rows, token_width)
        slot_max, slot_sum, slot_out = slot_partials(
            query_heads, key_rows, request, first_page, live_pages, page_counts, page_rows, latent
        )
        return (fold_slots(carry, request, slot_max, slot_sum, slot_out), None)

    initial = (
        jnp.full((request_count, query_count, head_count), neg_floor, jnp.float32),
        jnp.zeros((request_count, query_count, head_count), jnp.float32),
        jnp.zeros((request_count, query_count, head_count, latent), jnp.float32),
    )
    (best, denom, numer), _unused = lax.scan(
        one_block, initial, jnp.arange(block_count, dtype=jnp.int32)
    )
    partial_value = numer.astype(jnp.bfloat16)
    device_count = lax.axis_size(KV)
    columns = head_count * latent // device_count
    first_column = lax.axis_index(KV) * columns
    local_head_count = max(1, columns // latent)
    repeat_count = min(columns, latent)
    first_head = first_column // latent

    def local_heads(stats):
        last_axis = stats.ndim - 1
        picked = lax.dynamic_slice_in_dim(stats, first_head, local_head_count, last_axis)
        return jnp.repeat(picked, repeat_count, axis=last_axis)

    pieces = cut_exchange(
        partial_value.reshape(1, request_count, query_count, head_count * latent), KV, 2, 3, 0
    )
    all_best, all_denom = sent_together((best[None], denom[None]), KV, 0, 1)
    highest = jnp.max(all_best, axis=0)
    shrink = jnp.exp(all_best - highest)
    total = jnp.sum(shrink * all_denom, axis=0)
    summed = jnp.sum(pieces.astype(jnp.float32) * local_heads(shrink), axis=0)
    attended = (summed / local_heads(total)).astype(jnp.bfloat16)
    lse = highest + jnp.log(total)
    return (attended, lse)


def solution(mesh):
    split = Mesh(mesh.devices.reshape(mesh.shape["rep"], 8, 8, 2), ("rep", "kv_0", "kv_1", "kv_2"))
    placed = (
        P("rep", None, KV),
        P(REP_KV, None, None),
        P("rep"),
        P(REP_KV),
        P(REP_KV),
        P(REP_KV),
        P(REP_KV, None),
    )
    return jax.shard_map(
        per_device,
        mesh=split,
        in_specs=placed,
        out_specs=(P("rep", None, KV), P("rep", None, None)),
        check_vma=False,
    )
```

profile of v0, /device:TPU:514, one launch (start us, length us, event | category | flops | bytes accessed | tf_op | source)
XLA Modules:
  0.0 374.7 jit_solution(14392008454774396073)
XLA Ops:
  7.2 43.3 %all-gather = bf16[128,3,288]{2,0,1:T(8,128)(2,1)} all-gather(bf16[16,3,288]{2,0,1:T(8,128)(2,1)} %param.9), channel_id=2, replica_groups=mesh['rep'=2,'kv_0'=8,'kv_1'=8,'kv_2'=2] {'kv_0'}, dimensions={0}, use_global_device_ids=true | all-gather | bytes 248832 | tf_op jit(solution)/shard_map/all_gather | solution.py:26
  50.7 44.3 %all-gather.5.cloned.1.call-done = bf16[64,16,3,288]{3,1,0,2:T(8,128)(2,1)} async-done(((bf16[8,16,3,288]{3,1,0,2:T(8,128)(2,1)}), bf16[64,16,3,288]{3,1,0,2:T(8,128)(2,1)}) %all-gather.5.cloned.1.call-update) | async-done | bytes 1769488 | tf_op jit(solution)/shard_map/all_gather | solution.py:26
  95.2 8.9 %copy.107 = bf16[256,16,576]{2,1,0:T(8,128)(2,1)} copy(bf16[256,16,576]{0,2,1:T(8,128)(2,1)} %param.10) | data formatting | bytes 9437184
  104.1 12.9 %all-gather.7.cloned.1.call-done = bf16[128,16,3,288]{3,1,0,2:T(8,128)(2,1)} async-done(((bf16[64,16,3,288]{3,1,0,2:T(8,128)(2,1)}), bf16[128,16,3,288]{3,1,0,2:T(8,128)(2,1)}) %all-gather.7.cloned.1.call-update) | async-done | bytes 3538960 | tf_op jit(solution)/shard_map/all_gather | solution.py:26
  119.9 3.3 copy.105
  123.2 8.2 %reshape_reshape.6 = bf16[16,3,64,576]{3,2,1,0:T(8,128)(2,1)} reshape(bf16[16,3,128,288]{3,2,1,0:T(8,128)(2,1)} %copy.105) | data formatting | bytes 7077888 | tf_op jit(solution)/shard_map/reshape;reshape | solution.py:126
  131.5 81.9 %while.17 = (s32[]{:T(128)}, f32[16,3,64]{2,0,1:T(8,128)S(1)}, f32[16,3,64]{2,0,1:T(8,128)S(1)}, f32[16,3,64,512]{3,0,2,1:T(8,128)}, s32[4]{0:T(128)S(1)}, /*ind...) while((s32[]{:T(128)}, f32[16,3,64]{2,0,1:T(8,128)S(1)}, ...), condition=%wide.region_5.6_spmd.clone, body=%wide.region_0.5_spmd.clone.sunk | while | flops 586757760 | bytes 34555300 | solution.py:152
  136.8 3.3 gather_fusion.1
  144.5 5.6 %fusion.49 = f32[16,3,64,512]{3,0,2,1:T(8,128)} fusion(f32[16,3,64,512]{3,0,2,1:T(8,128)} %get-tuple-element.435, f32[16,3,64]{0,2,1:T(8,128)S(1)} %copy.150, pred[]{:T(512)S(6)} %compare.12, f32[8,3,64,512]{3,2,1,0:T(8,128)S(1)} %convolution_multiply_fusion.3, s32[8]{0:T(128)S(1)} %get-tuple-element.408), kind=kOutput, calls=%fused_computation.3.clone.1 | convolution fusion | flops 155713664 | bytes 15740961 | tf_op jit(solution)/shard_map/while/body/eval_jaxpr/gr,gqhc->rqhc/dot_general | solution.py:113
  155.4 3.3 gather_fusion.1
  163.1 8.1 %fusion.49 = f32[16,3,64,512]{3,0,2,1:T(8,128)} fusion(f32[16,3,64,512]{3,0,2,1:T(8,128)} %get-tuple-element.435, f32[16,3,64]{0,2,1:T(8,128)S(1)} %copy.150, pred[]{:T(512)S(6)} %compare.12, f32[8,3,64,512]{3,2,1,0:T(8,128)S(1)} %convolution_multiply_fusion.3, s32[8]{0:T(128)S(1)} %get-tuple-element.408), kind=kOutput, calls=%fused_computation.3.clone.1 | convolution fusion | flops 155713664 | bytes 15740961 | tf_op jit(solution)/shard_map/while/body/eval_jaxpr/gr,gqhc->rqhc/dot_general | solution.py:113
  176.5 3.3 gather_fusion.1
  184.2 8.1 %fusion.49 = f32[16,3,64,512]{3,0,2,1:T(8,128)} fusion(f32[16,3,64,512]{3,0,2,1:T(8,128)} %get-tuple-element.435, f32[16,3,64]{0,2,1:T(8,128)S(1)} %copy.150, pred[]{:T(512)S(6)} %compare.12, f32[8,3,64,512]{3,2,1,0:T(8,128)S(1)} %convolution_multiply_fusion.3, s32[8]{0:T(128)S(1)} %get-tuple-element.408), kind=kOutput, calls=%fused_computation.3.clone.1 | convolution fusion | flops 155713664 | bytes 15740961 | tf_op jit(solution)/shard_map/while/body/eval_jaxpr/gr,gqhc->rqhc/dot_general | solution.py:113
  197.6 3.3 gather_fusion.1
  205.3 8.1 %fusion.49 = f32[16,3,64,512]{3,0,2,1:T(8,128)} fusion(f32[16,3,64,512]{3,0,2,1:T(8,128)} %get-tuple-element.435, f32[16,3,64]{0,2,1:T(8,128)S(1)} %copy.150, pred[]{:T(512)S(6)} %compare.12, f32[8,3,64,512]{3,2,1,0:T(8,128)S(1)} %convolution_multiply_fusion.3, s32[8]{0:T(128)S(1)} %get-tuple-element.408), kind=kOutput, calls=%fused_computation.3.clone.1 | convolution fusion | flops 155713664 | bytes 15740961 | tf_op jit(solution)/shard_map/while/body/eval_jaxpr/gr,gqhc->rqhc/dot_general | solution.py:113
  214.1 3.3 convert_element_type.19
  217.3 3.4 copy.108
  220.8 3.9 %reshape_reshape.7 = bf16[1,16,3,128,256]{4,3,2,1,0:T(8,128)(2,1)S(1)} reshape(bf16[16,3,64,512]{3,2,1,0:T(8,128)(2,1)} %copy.108) | data formatting | bytes 6291456 | tf_op jit(solution)/shard_map/reshape;reshape | solution.py:39
  228.1 15.6 %all-to-all-start.1 = ((bf16[128,1,8,3,256]{4,2,3,1,0:T(8,128)(2,1)}), bf16[128,1,8,3,256]{4,2,3,1,0:T(8,128)(2,1)S(1)}, u32[]{:S(2)}, u32[]{:S(2)}) async-start(bf16[128,1,8,3,256]{4,2,3,1,0:T(8,128)(2,1)} %copy.110), calls=%async_computation.1 | async-start | bytes 3145728 | tf_op jit(solution)/shard_map/all_to_all | solution.py:54
  245.7 39.9 %all-to-all-done.1 = bf16[128,1,8,3,256]{4,2,3,1,0:T(8,128)(2,1)S(1)} async-done(((bf16[128,1,8,3,256]{4,2,3,1,0:T(8,128)(2,1)}), bf16[128,1,8,3,256]{4,2,3,1,0:T(8,128)(2,1)S(1)}, u32[]{:S(2)}, u32[]{:S(2)}) %all-to-all-start.1) | async-done | bytes 1572896 | tf_op jit(solution)/shard_map/all_to_all | solution.py:54
  285.6 8.3 %all-to-all-start = ((bf16[128,1,8,3,256]{4,2,3,1,0:T(8,128)(2,1)}), bf16[128,1,8,3,256]{4,2,3,1,0:T(8,128)(2,1)}, u32[]{:S(2)}, u32[]{:S(2)}) async-start(bf16[128,1,8,3,256]{4,2,3,1,0:T(8,128)(2,1)} %copy.109), calls=%async_computation | async-start | bytes 3145728 | tf_op jit(solution)/shard_map/all_to_all | solution.py:54
  293.9 57.0 %all-gather.9.cloned.1.call-done = f32[128,32,3,64]{3,1,2,0:T(8,128)} async-done(((f32[1,32,3,64]{3,1,2,0:T(8,128)}), f32[128,32,3,64]{3,1,2,0:T(8,128)}) %all-gather.9.cloned.1.call-update) | async-done | bytes 3145744 | tf_op jit(solution)/shard_map/all_gather | solution.py:64
  350.9 5.1 %slice_reduce_fusion = (f32[16,3,64]{2,0,1:T(8,128)S(1)}, f32[128,16,3,64]{3,1,2,0:T(8,128)S(1)}, f32[128,16,3,64]{3,1,2,0:T(8,128)}) fusion(f32[128,32,3,64]{3,1,2,0:T(8,128)} %all-gather.9.cloned.1.call-done), kind=kLoop, calls=%fused_computation.61 | loop fusion | flops 390144 | bytes 6303744 | tf_op jit(solution)/shard_map/reduce_max | solution.py:172
  356.0 3.3 copy.128
  (168 shorter events, 54.0 us)
Async XLA Ops:
  7.2 87.8 %all-gather.5.cloned.1.call-start = ((), (), s32[]{:S(2)}) async-start(), calls=%async_computation.2 | async-start | bytes 2654208 | tf_op jit(solution)/shard_map/all_gather | solution.py:26
  50.6 66.4 %all-gather.7.cloned.1.call-start = ((), (), s32[]{:S(2)}) async-start(), calls=%async_computation.3 | async-start | bytes 7077888 | tf_op jit(solution)/shard_map/all_gather | solution.py:26
  95.1 255.8 %all-gather.9.cloned.1.call-start = ((), (), s32[]{:S(2)}) async-start(), calls=%async_computation.4 | async-start | bytes 6340608 | tf_op jit(solution)/shard_map/all_gather | solution.py:64
  123.2 8.3 %copy-start.4 = (s32[32,8]{0,1:T(8,128)S(1)}, s32[32,8]{0,1:T(8,128)}, u32[]{:S(2)}) copy-start(s32[32,8]{0,1:T(8,128)} %param.15) | copy-start | bytes 3076
  123.2 8.3 %copy-start.5 = (s32[32]{0:T(128)S(1)}, s32[32]{0:T(128)}, u32[]{:S(2)}) copy-start(s32[32]{0:T(128)} %param.12) | copy-start | bytes 388
  123.2 8.3 %copy-start.6 = (s32[32]{0:T(128)S(1)}, s32[32]{0:T(128)}, u32[]{:S(2)}) copy-start(s32[32]{0:T(128)} %param.14) | copy-start | bytes 388
  123.2 8.3 %copy-start.7 = (s32[32]{0:T(128)S(1)}, s32[32]{0:T(128)}, u32[]{:S(2)}) copy-start(s32[32]{0:T(128)} %param.13) | copy-start | bytes 388
  123.2 8.3 %copy-start.8 = (s32[16]{0:T(128)S(1)}, s32[16]{0:T(128)}, u32[]{:S(2)}) copy-start(s32[16]{0:T(128)} %param.11) | copy-start | bytes 196
  140.9 0.9 copy-start
  159.5 0.9 copy-start
  180.6 0.9 copy-start
  201.6 0.9 copy-start
  226.0 17.6 %copy-start.3 = (bf16[128,1,8,3,256]{4,0,3,2,1:T(8,128)(2,1)S(1)}, bf16[128,1,8,3,256]{4,0,3,2,1:T(8,128)(2,1)}, u32[]{:S(2)}) copy-start(bf16[128,1,8,3,256]{4,0,3,2,1:T(8,128)(2,1)} %get-tuple-element.325) | copy-start | bytes 4718596
  228.1 57.5 %all-to-all-start.1 = ((bf16[128,1,8,3,256]{4,2,3,1,0:T(8,128)(2,1)}), bf16[128,1,8,3,256]{4,2,3,1,0:T(8,128)(2,1)S(1)}, u32[]{:S(2)}, u32[]{:S(2)}) async-start(bf16[128,1,8,3,256]{4,2,3,1,0:T(8,128)(2,1)} %copy.110), calls=%async_computation.1 | async-start | bytes 3145728 | tf_op jit(solution)/shard_map/all_to_all | solution.py:54
  285.5 8.4 %copy-start.1 = (bf16[128,1,8,3,256]{4,2,3,1,0:T(8,128)(2,1)}, bf16[128,1,8,3,256]{4,2,3,1,0:T(8,128)(2,1)S(1)}, u32[]{:S(2)}) copy-start(bf16[128,1,8,3,256]{4,2,3,1,0:T(8,128)(2,1)S(1)} %all-to-all-done.1) | copy-start | bytes 4718596
  285.6 79.1 %all-to-all-start = ((bf16[128,1,8,3,256]{4,2,3,1,0:T(8,128)(2,1)}), bf16[128,1,8,3,256]{4,2,3,1,0:T(8,128)(2,1)}, u32[]{:S(2)}, u32[]{:S(2)}) async-start(bf16[128,1,8,3,256]{4,2,3,1,0:T(8,128)(2,1)} %copy.109), calls=%async_computation | async-start | bytes 3145728 | tf_op jit(solution)/shard_map/all_to_all | solution.py:54
  361.3 3.3 copy-start.2
Sparse Core Ops, SparseCore 0:
  50.8 44.1 all-gather.4
  96.8 20.1 all-gather.6
  214.2 136.6 all-gather.8
where the time goes:
time: 377 us; the launch traced here: 375 us
  waiting for transfers between devices  154 us (41%)
  local copies, waits for them, and re-layouts  74.6 us (20%)
  blocking collectives  43.3 us (11%)
  matrix products  42.2 us (11%)
  starting transfers between devices  24.1 us (6%)
  other arithmetic  19.4 us (5%)
  between operations  14 us (4%)
    all_gather x2, waiting for transfers between devices, gather_in_order(): blocks = lax.all_gather(blocks, axes[k], axis=0, tiled=True)  57.2 us
    all_gather x1, waiting for transfers between devices, sent_together(): lax.all_gather(both, axis, axis=dim, tiled=True)  57 us
    all_gather x1, blocking collectives, gather_in_order(): blocks = lax.all_gather(blocks, axes[k], axis=0, tiled=True)  43.3 us
    all_to_all x2, waiting for transfers between devices, cut_exchange(): lax.all_to_all(piece, axis, split_axis=0, concat_axis=0, tiled=True)  39.9 us
    dot_general x4, matrix products, fold_slots(): jnp.einsum('gr,gqhc->rqhc', member_float, factor[..., None] * slot_out, p...  30 us
    all_to_all x2, starting transfers between devices, cut_exchange(): lax.all_to_all(piece, axis, split_axis=0, concat_axis=0, tiled=True)  23.9 us
    unnamed x22, local copies, waits for them, and re-layouts  15.7 us
    gather x4, local copies, waits for them, and re-layouts, one_block(): cache[pages.reshape(-1)]  13.1 us
  transfers between devices with their start and end apart: 5, of which 4 were waited for; matrix products, arithmetic and copies ran while one was open for 10% of the time, Pallas kernels for 0%

commit v1 on v0

v1 whole, which is shorter than its diff:
```python
import functools

import jax
import jax.numpy as jnp
from jax import lax
from jax.experimental import pallas as pl
from jax.experimental.pallas import tpu as pltpu
from jax.sharding import Mesh
from jax.sharding import PartitionSpec as P

ROPE = 64
LANES = 128
KV = ("kv_0", "kv_1", "kv_2")
REP_KV = ("rep", "kv_0", "kv_1", "kv_2")
MESH_ID = pl.DeviceIdType.MESH

softmax_scale = 192.0 ** (-0.5)
neg_floor = -1e30
f32 = jnp.float32
bf16 = jnp.bfloat16


def offset_of(j):
    return (j + 1) // 2 * (2 * (j % 2) - 1)


def ring_places(n):
    x, y, c = (lax.axis_index(axis) for axis in KV)

    def first_peer(d):
        return {"kv_0": (x + d * (1 - c) + n) % n, "kv_1": (y + d * c + n) % n, "kv_2": c}

    def second_peer(d):
        return {"kv_0": (x + d * c + n) % n, "kv_1": (y + d * (1 - c) + n) % n, "kv_2": c}

    partner = {"kv_0": x, "kv_1": y, "kv_2": 1 - c}
    return x, y, c, first_peer, second_peer, partner


def greet(peers):
    barrier = pltpu.get_barrier_semaphore()
    for peer in peers:
        pl.semaphore_signal(barrier, inc=1, device_id=peer, device_id_type=MESH_ID)
    pl.semaphore_wait(barrier, len(peers))


def send(src, dst, send_sem, recv_sem, peer):
    return pltpu.make_async_remote_copy(
        src_ref=src, dst_ref=dst, send_sem=send_sem, recv_sem=recv_sem, device_id=peer, device_id_type=MESH_ID
    )


def gather_kernel(
    n, q_ref, g_ref, other, pair_send, pair_recv, first_send, first_recv, right_send, right_recv, left_send, left_recv,
    share_send, share_recv
):
    x, y, c, first_peer, second_peer, partner = ring_places(n)
    half = n // 2
    block_tiles = g_ref.shape[2]
    greet([first_peer(offset_of(j)) for j in range(1, n)] + [second_peer(1), second_peer(-1), partner])
    swap = send(q_ref, other, pair_send, pair_recv, partner)
    swap.start()
    swap.wait()

    def place(a, b):
        return ((x + a * (1 - c) + b * c + 2 * n) % n) * n + (y + a * c + b * (1 - c) + 2 * n) % n

    mine = place(0, 0)
    query_count = q_ref.shape[0]
    latent_tiles = q_ref.shape[2] // LANES - 1
    tiles = []
    rotary = []
    for i in range(query_count):
        for t in range(latent_tiles + 1):
            cols = pl.ds(t * LANES, LANES)
            tile = q_ref[i, :, cols].astype(f32) + other[i, :, cols].astype(f32)
            (tiles if t < latent_tiles else rotary).append(tile)
    tiles.append(rotary[0] + pltpu.roll(rotary[1], ROPE, 1))
    tiles.append(rotary[2])
    for t in range(block_tiles):
        g_ref[c, mine, t] = jnp.where(c == 0, tiles[t], tiles[block_tiles + t]).astype(bf16)

    def share(block):
        ref = g_ref.at[c, block]
        send(ref, ref, share_send, share_recv, partner).start()

    def to_right(block, index):
        ref = g_ref.at[c, block]
        send(ref, ref, right_send, right_recv.at[index], second_peer(1)).start()

    def to_left(block, index):
        ref = g_ref.at[c, block]
        send(ref, ref, left_send, left_recv.at[index], second_peer(-1)).start()

    own = g_ref.at[c, mine]
    for j in range(1, n):
        send(own, own, first_send, first_recv.at[j], first_peer(offset_of(j))).start()
    to_right(mine, 0)
    to_left(mine, 0)
    share(mine)

    def first_step(j, _):
        block = place(-offset_of(j), 0)
        ref = g_ref.at[c, block]
        send(ref, ref, first_send, first_recv.at[j], partner).wait_recv()
        to_right(block, j)
        to_left(block, j)
        share(block)
        return 0

    lax.fori_loop(1, n, first_step, 0)

    def take_right(s, j, forward):
        block = place(-offset_of(j), -s)
        ref = g_ref.at[c, block]
        send(ref, ref, right_send, right_recv.at[(s - 1) * n + j], partner).wait_recv()
        if forward:
            to_right(block, s * n + j)
        share(block)

    def take_left(s, j, forward):
        block = place(-offset_of(j), s)
        ref = g_ref.at[c, block]
        send(ref, ref, left_send, left_recv.at[(s - 1) * n + j], partner).wait_recv()
        if forward:
            to_left(block, s * n + j)
        share(block)

    for s in range(1, half + 1):
        if s == half:

            def last_step(j, _):
                take_right(half, j, False)
                take_left(half, j + half, False)
                return 0

            lax.fori_loop(0, half, last_step, 0)
        elif s == half - 1:

            def low_step(j, _):
                take_right(half - 1, j, True)
                take_left(half - 1, j, False)
                return 0

            def high_step(j, _):
                take_right(half - 1, j, False)
                take_left(half - 1, j, True)
                return 0

            lax.fori_loop(0, half, low_step, 0)
            lax.fori_loop(half, n, high_step, 0)
        else:

            def mid_step(j, _, s=s):
                take_right(s, j, True)
                take_left(s, j, True)
                return 0

            lax.fori_loop(0, n, mid_step, 0)

    ring_blocks = n * (half - 1) + half
    some = g_ref.at[c, pl.ds(0, n - 1)]
    send(some, some, first_send, first_recv.at[0], partner).wait_send()
    some = g_ref.at[c, pl.ds(0, ring_blocks)]
    send(some, some, right_send, first_recv.at[0], partner).wait_send()
    send(some, some, left_send, first_recv.at[0], partner).wait_send()
    send(g_ref.at[c], g_ref.at[c], share_send, share_recv, partner).wait_send()
    send(g_ref.at[1 - c], g_ref.at[1 - c], share_send, share_recv, partner).wait_recv()


def gather_queries(q, n):
    query_count, requests, width = q.shape
    block_tiles = (query_count * (width // LANES - 1) + 2) // 2
    dma = pltpu.SemaphoreType.DMA
    return pl.pallas_call(
        functools.partial(gather_kernel, n),
        out_shape=jax.ShapeDtypeStruct((2, n * n, block_tiles, requests, LANES), bf16),
        in_specs=[pl.BlockSpec(memory_space=pltpu.VMEM)],
        out_specs=pl.BlockSpec(memory_space=pltpu.VMEM),
        scratch_shapes=[
            pltpu.VMEM(q.shape, bf16),
            dma, dma, dma, dma((n,)), dma, dma((n * n // 2,)), dma, dma((n * n // 2,)), dma, dma,
        ],
        compiler_params=pltpu.CompilerParams(collective_id=0, has_side_effects=True),
        name="gather_queries",
    )(q)


def attend_kernel(
    n, latent, g_ref, cache_ref, pages_ref, req, start, live, counts, part_ref, stat_ref, cache_v, cache_sem, sel, keys_v,
    q32, qr, acc, mrep, lrep, place, shift
):
    heads = n * n
    block_tiles, requests = g_ref.shape[2], g_ref.shape[3]
    span, slots = pages_ref.shape
    page_rows, width, page_count = cache_v.shape
    latent_tiles = latent // LANES
    query_count = part_ref.shape[2]
    rows = heads * query_count
    fetch = pltpu.make_async_copy(cache_ref, cache_v, cache_sem)
    fetch.start()

    def spread(h, _):
        def tile(t):
            return g_ref[t // block_tiles, h, t % block_tiles].astype(f32)

        for i in range(query_count):
            at = pl.ds(pl.multiple_of((h * query_count + i) * requests, requests), requests)
            for t in range(latent_tiles):
                q32[t, at, :] = tile(i * latent_tiles + t)
            rotary = tile(query_count * latent_tiles + i // 2)
            q32[latent_tiles, at, :] = pltpu.roll(rotary, ROPE, 1) if i % 2 else rotary
        return 0

    lax.fori_loop(0, heads, spread, 0)
    for r in range(requests):
        for t in range(latent_tiles + 1):
            qr[r, :, pl.ds(t * LANES, LANES)] = q32[t, pl.ds(r, rows, stride=requests), :].astype(bf16)

    acc[...] = jnp.zeros_like(acc)
    mrep[...] = jnp.full_like(mrep, neg_floor)
    lrep[...] = jnp.zeros_like(lrep)
    lane = lax.broadcasted_iota(jnp.int32, (rows, LANES), 1)
    place[...] = lane % span * page_rows + lane // span
    shift[...] = place[...] - lax.broadcasted_iota(jnp.int32, (rows, LANES), 0) % query_count
    page_lane = lax.broadcasted_iota(jnp.int32, (span, page_count), 1)
    for s in range(0, slots, 2):
        pair = [jnp.where(pages_ref[:, s + u : s + u + 1] == page_lane, 1.0, 0.0) for u in range(2)]
        sel[pl.ds(s * span, 2 * span), :] = jnp.concatenate(pair, axis=0).astype(bf16)
    fetch.wait()

    def pick(t, _):
        both = [
            lax.dot_general(
                sel[...], cache_v[2 * t + u], (((1,), (1,)), ((), ())), preferred_element_type=f32
            )
            for u in range(2)
        ]
        for s in range(slots):
            chunk = jnp.concatenate([one[s * span : (s + 1) * span] for one in both], axis=0)
            keys_v[s, pl.ds(pl.multiple_of(t * 2 * span, 2 * span), 2 * span), :] = chunk.astype(bf16)
        return 0

    lax.fori_loop(0, page_rows // 2, pick, 0)

    def slot_step(s, _):
        r = req[s]
        keys = keys_v[s]
        scores = (
            lax.dot_general(
                qr[r, :, :width], keys, (((1,), (1,)), ((), ())), preferred_element_type=f32
            )
            * softmax_scale
        )
        limit = (counts[r] - start[s]) * page_rows - (query_count - 1)
        visible = (place[...] < live[s] * page_rows) & (shift[...] < limit)
        slot_max = jnp.max(jnp.where(visible, scores, neg_floor), axis=1, keepdims=True)
        weights = jnp.exp(jnp.where(visible, scores - slot_max, neg_floor))
        slot_sum = jnp.sum(weights, axis=1, keepdims=True)
        slot_out = jnp.dot(weights.astype(bf16), keys[:, :latent], preferred_element_type=f32)
        at = pl.ds(r, rows, stride=requests)
        old = mrep[at, :]
        new = jnp.maximum(old, slot_max)
        kept = jnp.exp(old - new)
        added = jnp.exp(slot_max - new)
        mrep[at, :] = new
        lrep[at, :] = lrep[at, :] * kept + added * slot_sum
        for t in range(latent_tiles):
            acc[t, at, :] = acc[t, at, :] * kept + slot_out[:, t * LANES : (t + 1) * LANES] * added
        return 0

    lax.fori_loop(0, slots, slot_step, 0)

    def put(h, _):
        turned = h % n * n + h // n
        for i in range(query_count):
            at = pl.ds(pl.multiple_of((h * query_count + i) * requests, requests), requests)
            for t in range(latent_tiles):
                side = t * 2 // latent_tiles
                cols = pl.ds((t - side * latent_tiles // 2) * LANES, LANES)
                part_ref[side, h if side == 0 else turned, i, :, cols] = acc[t, at, :].astype(bf16)
        return 0

    lax.fori_loop(0, heads, put, 0)
    head_lane = lax.broadcasted_iota(jnp.int32, (heads, LANES), 1)
    stats = jnp.zeros((heads, LANES), f32)
    for i in range(query_count):
        for r in range(requests):
            at = pl.ds(i * requests + r, heads, stride=query_count * requests)
            stats = jnp.where(head_lane == i * requests + r, mrep[at, :], stats)
            stats = jnp.where(head_lane == (query_count + i) * requests + r, lrep[at, :], stats)
    stat_ref[0] = stats
    for a in range(n):
        stat_ref[1, pl.ds(a * n, n), :] = stat_ref[0, pl.ds(a, n, stride=n), :]


def attend(gathered, cache, pages, tables, n, query_count, latent):
    page_rows, key_width, page_count = cache.shape
    span, slots = pages.shape
    heads = n * n
    requests = gathered.shape[3]
    rows = heads * query_count
    vmem = pl.BlockSpec(memory_space=pltpu.VMEM)
    smem = pl.BlockSpec(memory_space=pltpu.SMEM)
    width = (latent // LANES + 1) * LANES
    return pl.pallas_call(
        functools.partial(attend_kernel, n, latent),
        out_shape=(
            jax.ShapeDtypeStruct((2, heads, query_count, requests, latent // 2), bf16),
            jax.ShapeDtypeStruct((2, heads, LANES), f32),
        ),
        in_specs=[vmem, pl.BlockSpec(memory_space=pl.ANY), vmem] + [smem] * 4,
        out_specs=(vmem, vmem),
        scratch_shapes=[
            pltpu.VMEM(cache.shape, bf16),
            pltpu.SemaphoreType.DMA,
            pltpu.VMEM((slots * span, page_count), bf16),
            pltpu.VMEM((slots, page_rows * span, key_width), bf16),
            pltpu.VMEM((width // LANES, rows * requests, LANES), f32),
            pltpu.VMEM((requests, rows, width), bf16),
            pltpu.VMEM((latent // LANES, rows * requests, LANES), f32),
            pltpu.VMEM((rows * requests, LANES), f32),
            pltpu.VMEM((rows * requests, LANES), f32),
            pltpu.VMEM((rows, LANES), jnp.int32),
            pltpu.VMEM((rows, LANES), jnp.int32),
        ],
        name="attend",
    )(gathered, cache, pages, *tables)


def combine_kernel(
    n, part_ref, stat_ref, out_ref, lse_ref, pair_part, pair_stat, f_mine, f_pair, chip_part, chip_stat, ring_part,
    ring_stat, f_ring, total, col_send_part, col_stat_send, col_part, col_stat, f_col, lse_send,
    sem_pair_stat, sem_pair_part, sem_stat_a, sem_part_a, sem_stat_b, sem_part_b, sem_lse
):
    x, y, c, first_peer, second_peer, partner = ring_places(n)
    a_here = x * (1 - c) + y * c
    b_here = y * (1 - c) + x * c
    _h, query_count, requests, cols = chip_part.shape[1:]
    m_lanes = query_count * requests
    greet(
        [first_peer(offset_of(j)) for j in range(1, n)] + [second_peer(offset_of(j)) for j in range(1, n)] + [partner]
    )
    order = list(range(n - 1, -1, -1))

    def a_at(d):
        return (a_here + d + n) % n

    def b_at(d):
        return (b_here + d + n) % n

    stat_swap = send(stat_ref.at[1 - c], pair_stat, sem_pair_stat.at[0], sem_pair_stat.at[1], partner)
    stat_swap.start()
    for j in order:
        a_pair = (b_here + offset_of(j) + n) % n
        send(
            part_ref.at[1 - c, a_pair], pair_part.at[a_pair], sem_pair_part.at[0, j], sem_pair_part.at[1, j], partner
        ).start()
    stat_swap.wait()

    lane8 = lax.broadcasted_iota(jnp.int32, (n, LANES), 1)
    lane16 = lax.broadcasted_iota(jnp.int32, (requests, LANES), 1)
    row16 = lax.broadcasted_iota(jnp.int32, (requests, LANES), 0)

    def column(row, base):
        picked = jnp.where(lane16 == row16 + base, jnp.broadcast_to(row, (requests, LANES)), 0.0)
        return jnp.sum(picked, axis=1, keepdims=True)

    def merged(all_stats):
        best = all_stats[0]
        for one in all_stats[1:]:
            best = jnp.maximum(best, one)
        factors = [jnp.exp(one - best) for one in all_stats]
        denom = 0.0
        for factor, one in zip(factors, all_stats):
            denom = denom + pltpu.roll(factor, m_lanes, 1) * one
        return factors, jnp.where(lane8 < m_lanes, best, denom)

    for a in range(n):
        factors, stats = merged([stat_ref[c, a], pair_stat[a]])
        f_mine[a] = factors[0]
        f_pair[a] = factors[1]
        chip_stat[a] = stats
    for j in order[:-1]:
        send(
            chip_stat.at[a_at(offset_of(j))], ring_stat.at[j], sem_stat_a.at[0, j], sem_stat_a.at[1, j],
            first_peer(offset_of(j)),
        ).start()
    ring_stat[0] = chip_stat[a_here]

    def pair_chunk(j, _):
        a_pair = (b_here + offset_of(j) + n) % n
        a = a_at(offset_of(j))
        send(
            part_ref.at[1 - c, a_pair], pair_part.at[a], sem_pair_part.at[0, j], sem_pair_part.at[1, j], partner
        ).wait()
        f_m = f_mine[a]
        f_p = f_pair[a]
        for b in range(n):
            for i in range(query_count):
                mine = part_ref[c, a, b, i].astype(f32) * column(f_m[b : b + 1], i * requests)
                theirs = pair_part[a, b, i].astype(f32) * column(f_p[b : b + 1], i * requests)
                chip_part[a, b, i] = (mine + theirs).astype(bf16)
        return a

    for j in order:
        a = pair_chunk(j, 0)
        if j:
            send(
                chip_part.at[a], ring_part.at[j], sem_part_a.at[0, j], sem_part_a.at[1, j], first_peer(offset_of(j))
            ).start()

    for j in range(1, n):
        send(
            chip_stat.at[a_here], ring_stat.at[j], sem_stat_a.at[0, j], sem_stat_a.at[1, j], first_peer(offset_of(j))
        ).wait()
    factors, stats = merged([ring_stat[j] for j in range(n)])
    for j in range(n):
        f_ring[j] = factors[j]
    col_stat_send[...] = stats
    for j in order[:-1]:
        send(
            col_stat_send, col_stat.at[j], sem_stat_b.at[0, j], sem_stat_b.at[1, j], second_peer(offset_of(j))
        ).start()
    col_stat[0] = stats
    for j in range(1, n):
        send(
            col_stat_send, col_stat.at[j], sem_stat_b.at[0, j], sem_stat_b.at[1, j], second_peer(offset_of(j))
        ).wait()
    factors, stats = merged([col_stat[j] for j in range(n)])
    for j in range(n):
        f_col[j] = factors[j]
    f_col[n] = stats
    lse = stats + jnp.log(pltpu.roll(jnp.where(lane8 < m_lanes, 1.0, stats), LANES - m_lanes, 1))
    lse_send[...] = lse
    lse_ref[a_here] = lse
    for j in range(1, n):
        send(
            lse_send, lse_ref.at[a_here], sem_lse.at[0, j], sem_lse.at[1, j], first_peer(offset_of(j))
        ).start()

    for j in range(n):
        if j:
            send(
                chip_part.at[a_here], ring_part.at[j], sem_part_a.at[0, j], sem_part_a.at[1, j],
                first_peer(offset_of(j)),
            ).wait()
        factor = f_ring[j]
        for b in range(n):
            for i in range(query_count):
                scale = column(factor[b : b + 1], i * requests)
                if j == 0:
                    total[b, i] = chip_part[a_here, b, i].astype(f32) * scale
                elif j < n - 1:
                    total[b, i] = total[b, i] + ring_part[j, b, i].astype(f32) * scale
                else:
                    col_send_part[b, i] = (total[b, i] + ring_part[j, b, i].astype(f32) * scale).astype(bf16)
    for j in order[:-1]:
        send(
            col_send_part.at[b_at(offset_of(j))], col_part.at[j], sem_part_b.at[0, j], sem_part_b.at[1, j],
            second_peer(offset_of(j)),
        ).start()
    sums = [0.0] * query_count
    for j in range(n):
        if j:
            send(
                col_send_part.at[b_here], col_part.at[j], sem_part_b.at[0, j], sem_part_b.at[1, j],
                second_peer(offset_of(j)),
            ).wait()
        row = f_col[j, pl.ds(b_here, 1), :]
        for i in range(query_count):
            block = col_send_part[b_here, i] if j == 0 else col_part[j, i]
            sums[i] = sums[i] + block.astype(f32) * column(row, i * requests)
    row = f_col[n, pl.ds(b_here, 1), :]
    for i in range(query_count):
        out_ref[i] = (sums[i] / column(row, m_lanes + i * requests)).astype(bf16)
    for j in range(1, n):
        a_from = a_at(-offset_of(j))
        send(
            lse_send, lse_ref.at[a_from], sem_lse.at[0, j], sem_lse.at[1, j], first_peer(offset_of(j))
        ).wait()


def combine(part, stat, n):
    _two, heads, query_count, requests, cols = part.shape
    part = part.reshape(2, n, n, query_count, requests, cols)
    stat = stat.reshape(2, n, n, LANES)
    vmem = pl.BlockSpec(memory_space=pltpu.VMEM)
    dma = pltpu.SemaphoreType.DMA
    block = (n, n, query_count, requests, cols)
    one = (n, query_count, requests, cols)
    return pl.pallas_call(
        functools.partial(combine_kernel, n),
        out_shape=(
            jax.ShapeDtypeStruct((query_count, requests, cols), bf16),
            jax.ShapeDtypeStruct((n, n, LANES), f32),
        ),
        in_specs=[vmem, vmem],
        out_specs=(vmem, vmem),
        scratch_shapes=[
            pltpu.VMEM(block, bf16),
            pltpu.VMEM((n, n, LANES), f32),
            pltpu.VMEM((n, n, LANES), f32),
            pltpu.VMEM((n, n, LANES), f32),
            pltpu.VMEM(block, bf16),
            pltpu.VMEM((n, n, LANES), f32),
            pltpu.VMEM(block, bf16),
            pltpu.VMEM((n, n, LANES), f32),
            pltpu.VMEM((n, n, LANES), f32),
            pltpu.VMEM(one, f32),
            pltpu.VMEM(one, bf16),
            pltpu.VMEM((n, LANES), f32),
            pltpu.VMEM(one, bf16),
            pltpu.VMEM((n, n, LANES), f32),
            pltpu.VMEM((n + 1, n, LANES), f32),
            pltpu.VMEM((n, LANES), f32),
            dma((2,)),
            dma((2, n)), dma((2, n)), dma((2, n)), dma((2, n)), dma((2, n)), dma((2, n)),
        ],
        compiler_params=pltpu.CompilerParams(collective_id=1, has_side_effects=True),
        name="combine",
    )(part, stat)


def per_device(n, queries, cache, page_counts, slot_request, slot_start, slot_live, slot_pages):
    requests, query_count, share = queries.shape
    width = cache.shape[2]
    latent = width - ROPE
    core = lax.axis_index(KV[2])
    turned = jnp.transpose(queries, (1, 0, 2))
    padded = (latent // LANES + 1) * LANES
    low = jnp.pad(turned, ((0, 0), (0, 0), (0, padded - share)))
    high = jnp.pad(turned, ((0, 0), (0, 0), (share, padded - 2 * share)))
    q = jnp.where(core == 0, low, high)
    gathered = gather_queries(q, n)
    tables = (slot_request, slot_start, slot_live, page_counts)
    turned_cache = jnp.transpose(cache, (1, 2, 0))
    part, stat = attend(gathered, turned_cache, slot_pages.T, tables, n, query_count, latent)
    out, lse = combine(part, stat, n)
    attended = jnp.transpose(out, (1, 0, 2))
    lse = jnp.where(core == 0, lse, jnp.swapaxes(lse, 0, 1))
    lse = lse.reshape(n * n, LANES)[:, : query_count * requests].reshape(n * n, query_count, requests)
    return attended, jnp.transpose(lse, (2, 1, 0))


def solution(mesh):
    n = round((mesh.shape["kv"] // 2) ** 0.5)
    split = Mesh(mesh.devices.reshape(mesh.shape["rep"], n, n, 2), REP_KV)
    placed = (
        P("rep", None, KV),
        P(REP_KV, None, None),
        P("rep"),
        P(REP_KV),
        P(REP_KV),
        P(REP_KV),
        P(REP_KV, None),
    )
    return jax.shard_map(
        functools.partial(per_device, n),
        mesh=split,
        in_specs=placed,
        out_specs=(P("rep", None, KV), P("rep", None, None)),
        check_vma=False,
    )
```

time: 377 us -> 131 us (0.35)
  waiting for transfers between devices: 154 us -> 0 us
  Pallas kernels: 0 us -> 124 us
  local copies, waits for them, and re-layouts: 74.6 us -> 2.03 us
  blocking collectives: 43.3 us -> 0 us
  matrix products: 42.2 us -> 0 us
  starting transfers between devices: 24.1 us -> 0 us
  other arithmetic: 19.4 us -> 2.4 us
  between operations: 14 us -> 0.66 us
    pallas_call x0 -> x3, Pallas kernels: none -> 124 us  [the longest x1 46 us: gather_queries(): pl.pallas_call(functools.partial(gather_kernel, n), out_shape=jax.ShapeDt...]
    all_gather x3 -> x0, waiting for transfers between devices: 114 us -> none  [the longest x2 57.2 us: gather_in_order(): blocks = lax.all_gather(blocks, axes[k], axis=0, tiled=True)]
    all_gather x1 -> x0, blocking collectives: 43.3 us -> none  [gather_in_order(): blocks = lax.all_gather(blocks, axes[k], axis=0, tiled=True)]
    dot_general x20 -> x0, matrix products: 42.2 us -> none  [the longest x4 30 us: fold_slots(): jnp.einsum('gr,gqhc->rqhc', member_float, factor[..., None] * slot_out, p...]
    all_to_all x2 -> x0, waiting for transfers between devices: 39.9 us -> none  [cut_exchange(): lax.all_to_all(piece, axis, split_axis=0, concat_axis=0, tiled=True)]
    gather x8 -> x0, local copies, waits for them, and re-layouts: 25.2 us -> none  [the longest x4 13.1 us: one_block(): cache[pages.reshape(-1)]]
    all_to_all x2 -> x0, starting transfers between devices: 23.9 us -> none  [cut_exchange(): lax.all_to_all(piece, axis, split_axis=0, concat_axis=0, tiled=True)]
    unnamed x22 -> x1, local copies, waits for them, and re-layouts: 15.7 us -> 1.35 us
  transfers between devices with their start and end apart: 5 -> 0, of which waited for: 4 -> 0; matrix products, arithmetic and copies ran while one was open for 10% -> 0% of each run, Pallas kernels for 0% -> 0%
where the time goes in v1:
time: 131 us; the launch traced here: 129 us
  Pallas kernels  124 us (95%)
  other arithmetic  2.4 us (2%)
  local copies, waits for them, and re-layouts  2.03 us (2%)
    pallas_call x1, Pallas kernels, gather_queries(): pl.pallas_call(functools.partial(gather_kernel, n), out_shape=jax.ShapeDt...  46 us
    pallas_call x1, Pallas kernels, attend(): pl.pallas_call(functools.partial(attend_kernel, n, latent), out_shape=(ja...  43.7 us
    pallas_call x1, Pallas kernels, combine(): pl.pallas_call(functools.partial(combine_kernel, n), out_shape=(jax.Shape...  34.6 us

profile of v1, /device:TPU:514, one launch (start us, length us, event | category | flops | bytes accessed | tf_op | source)
XLA Modules:
  0.0 129.5 jit_solution(15554953334077033750)
XLA Ops:
  0.6 1.6 %pad_select_fusion.q_ref = bf16[3,16,640]{2,1,0:T(8,128)(2,1)} fusion(bf16[3,16,288]{2,1,0:T(8,128)(2,1)} %bitcast.20, pred[]{:T(512)S(6)} %eq.4), kind=kLoop, calls=%fused_computation | loop fusion | flops 30720 | bytes 89089 | tf_op jit(solution)/shard_map/jit(_where)/select_n | solution.py:534
  2.2 46.0 %gather_queries.1.g_ref = bf16[2,64,7,16,128]{4,3,2,1,0:T(8,128)(2,1)} custom-call(bf16[3,16,640]{2,1,0:T(8,128)(2,1)} %pad_select_fusion.q_ref), custom_call_target="tpu_custom_call" | custom-call | tf_op jit(solution)/shard_map/gather_queries/pallas_call | solution.py:175
  48.2 43.7 %attend.1 = (bf16[2,64,3,16,256]{4,3,2,1,0:T(8,128)(2,1)}, f32[2,64,128]{2,1,0:T(8,128)}) custom-call(bf16[2,64,7,16,128]{4,3,2,1,0:T(8,128)(2,1)} %gather_queries.1.g_ref, bf16[16,576,256]{2,1,0:T(8,128)(2,1)} %bitcast.16, s32[8,32]{1,0:T(8,128)} %bitcast.23, s32[32]{0:T(128)} %req.1, s32[32]{0:T(128)} %start.1, s32[32]{0:T(128)} %live.1, s32[16]{0:T(128)} %counts.1), custom_call_target="tpu_custom_call" | custom-call | tf_op jit(solution)/shard_map/attend/pallas_call | solution.py:306
  91.9 34.6 %combine.1 = (bf16[3,16,256]{2,1,0:T(8,128)(2,1)}, f32[8,8,128]{2,1,0:T(8,128)}) custom-call(bf16[2,8,8,3,16,256]{5,4,3,2,1,0:T(8,128)(2,1)} %bitcast.17, f32[2,8,8,128]{3,2,1,0:T(8,128)} %bitcast.19), custom_call_target="tpu_custom_call" | custom-call | tf_op jit(solution)/shard_map/combine/pallas_call | solution.py:492
  126.6 0.8 fusion
  127.4 0.7 copy.10
  128.1 1.3 %copy.13 = bf16[16,3,256]{2,0,1:T(8,128)(2,1)} copy(bf16[16,3,256]{2,0,1:T(8,128)(2,1)} %bitcast.22) | data formatting | bytes 49152

commit v2 on v1

v2 whole, which is shorter than its diff:
```python
import functools
from types import SimpleNamespace

import jax
import jax.numpy as jnp
from jax import lax
from jax.experimental import pallas as pl
from jax.experimental.pallas import tpu as pltpu
from jax.sharding import Mesh
from jax.sharding import PartitionSpec as P

ROPE = 64
LANES = 128
KV = ("kv_0", "kv_1", "kv_2")
REP_KV = ("rep", "kv_0", "kv_1", "kv_2")
MESH_ID = pl.DeviceIdType.MESH

softmax_scale = 192.0 ** (-0.5)
neg_floor = -1e30
f32 = jnp.float32
bf16 = jnp.bfloat16


def offset_of(j):
    return (j + 1) // 2 * (2 * (j % 2) - 1)


def ring_places(n):
    x, y, c = (lax.axis_index(axis) for axis in KV)

    def first_peer(d):
        return {"kv_0": (x + d * (1 - c) + n) % n, "kv_1": (y + d * c + n) % n, "kv_2": c}

    def second_peer(d):
        return {"kv_0": (x + d * c + n) % n, "kv_1": (y + d * (1 - c) + n) % n, "kv_2": c}

    partner = {"kv_0": x, "kv_1": y, "kv_2": 1 - c}
    return x, y, c, first_peer, second_peer, partner


def greet(peers):
    barrier = pltpu.get_barrier_semaphore()
    for peer in peers:
        pl.semaphore_signal(barrier, inc=1, device_id=peer, device_id_type=MESH_ID)
    pl.semaphore_wait(barrier, len(peers))


def send(src, dst, send_sem, recv_sem, peer):
    return pltpu.make_async_remote_copy(
        src_ref=src, dst_ref=dst, send_sem=send_sem, recv_sem=recv_sem, device_id=peer, device_id_type=MESH_ID
    )


def decode_kernel(n, latent, names, *refs):
    v = SimpleNamespace(**dict(zip(names, refs)))
    x, y, c, first_peer, second_peer, partner = ring_places(n)
    fetch = pltpu.make_async_copy(v.cache, v.cache_v, v.cache_sem)
    fetch.start()
    greet(
        [first_peer(offset_of(j)) for j in range(1, n)] + [second_peer(offset_of(j)) for j in range(1, n)] + [partner]
    )
    gather_part(n, v, x, y, c, first_peer, second_peer, partner, fetch)
    attend_part(n, latent, v, c)
    combine_part(n, v, x, y, c, first_peer, second_peer, partner)


def attention_tables(n, v):
    slots = v.req.shape[0]
    requests = v.counts.shape[0]
    requested = [v.req[s] for s in range(slots)]

    def find_before(s, _):
        mine = v.req[s]
        found = slots
        for t in range(slots):
            found = jnp.where((requested[t] == mine) & (t < s), t, found)
        v.before[s] = found
        return 0

    def find_last(r, _):
        found = slots
        for t in range(slots):
            found = jnp.where(requested[t] == r, t, found)
        v.last[r] = found
        return 0

    lax.fori_loop(0, slots, find_before, 0)
    lax.fori_loop(0, requests, find_last, 0)


def attention_constants(n, v):
    span, slots = v.pages.shape
    page_rows, _width, page_count = v.cache_v.shape
    requests = v.counts.shape[0]
    heads = n * n
    rows = v.place.shape[0]
    group = min(requests, heads)
    size = requests * group
    lane = lax.broadcasted_iota(jnp.int32, (rows, LANES), 1)
    v.place[...] = lane % span * page_rows + lane // span
    v.shift[...] = v.place[...] - lax.broadcasted_iota(jnp.int32, (rows, LANES), 0) // heads
    turn_row = lax.broadcasted_iota(jnp.int32, (size, size), 0)
    turn_col = lax.broadcasted_iota(jnp.int32, (size, size), 1)
    from_heads = jnp.where(turn_col == turn_row % group * requests + turn_row // group, 1.0, 0.0)
    v.turn[0] = from_heads.astype(bf16)
    to_heads = jnp.where(turn_row == turn_col % group * requests + turn_col // group, 1.0, 0.0)
    v.turn[1] = to_heads.astype(bf16)
    page_lane = lax.broadcasted_iota(jnp.int32, (span, page_count), 1)
    for s in range(0, slots, 2):
        pair = [jnp.where(v.pages[:, s + u : s + u + 1] == page_lane, 1.0, 0.0) for u in range(2)]
        v.sel[pl.ds(s * span, 2 * span), :] = jnp.concatenate(pair, axis=0).astype(bf16)
    v.acc[slots] = jnp.zeros(v.acc.shape[1:], f32)
    v.mrep[slots] = jnp.full(v.mrep.shape[1:], neg_floor, f32)
    v.lrep[slots] = jnp.zeros(v.lrep.shape[1:], f32)


def pick_rows(v, t):
    span, slots = v.pages.shape
    both = [
        lax.dot_general(v.sel[...], v.cache_v[2 * t + u], (((1,), (1,)), ((), ())), preferred_element_type=f32)
        for u in range(2)
    ]
    for s in range(slots):
        chunk = jnp.concatenate([one[s * span : (s + 1) * span] for one in both], axis=0)
        v.keys_v[s, pl.ds(pl.multiple_of(t * 2 * span, 2 * span), 2 * span), :] = chunk.astype(bf16)


def gather_part(n, v, x, y, c, first_peer, second_peer, partner, fetch):
    half = n // 2
    block_tiles = v.gathered.shape[2]
    g_ref, q_ref, other = v.gathered, v.q, v.other
    swap = send(q_ref, other, v.pair_send, v.pair_recv, partner)
    swap.start()
    swap.wait()

    def place(a, b):
        return ((x + a * (1 - c) + b * c + 2 * n) % n) * n + (y + a * c + b * (1 - c) + 2 * n) % n

    mine = place(0, 0)
    query_count, requests, held = q_ref.shape
    lane = lax.broadcasted_iota(jnp.int32, (requests, LANES), 1)
    tail = held % LANES
    pad = jnp.zeros((requests, LANES - tail), f32)
    tiles = []
    rotary = []
    for i in range(query_count):
        here = q_ref[i].astype(f32)
        there = other[i].astype(f32)
        low = jnp.concatenate([jnp.where(c == 0, here, there), pad], axis=1)
        high = jnp.concatenate([jnp.where(c == 0, there, here), pad], axis=1)
        full = held // LANES
        low = [low[:, t * LANES : (t + 1) * LANES] for t in range(full + 1)]
        high = [pltpu.roll(high[:, t * LANES : (t + 1) * LANES], tail, 1) for t in range(full + 1)]
        tiles += low[:full]
        left = low[full]
        for t in range(full):
            tiles.append(jnp.where(lane < tail, left, high[t]))
            left = high[t]
        rotary.append(jnp.where(lane < tail, left, jnp.where(lane < 2 * tail, high[full], 0.0)))
    tiles.append(rotary[0] + pltpu.roll(rotary[1], ROPE, 1))
    tiles.append(rotary[2])
    for t in range(block_tiles):
        g_ref[c, mine, t] = jnp.where(c == 0, tiles[t], tiles[block_tiles + t]).astype(bf16)

    def share(block):
        ref = g_ref.at[c, block]
        send(ref, ref, v.share_send, v.share_recv, partner).start()

    def to_right(block, index):
        ref = g_ref.at[c, block]
        send(ref, ref, v.right_send, v.right_recv.at[index], second_peer(1)).start()

    def to_left(block, index):
        ref = g_ref.at[c, block]
        send(ref, ref, v.left_send, v.left_recv.at[index], second_peer(-1)).start()

    own = g_ref.at[c, mine]
    for j in range(1, n):
        send(own, own, v.first_send, v.first_recv.at[j], first_peer(offset_of(j))).start()
    to_right(mine, 0)
    to_left(mine, 0)
    share(mine)

    def first_step(j, _):
        block = place(-offset_of(j), 0)
        ref = g_ref.at[c, block]
        send(ref, ref, v.first_send, v.first_recv.at[j], partner).wait_recv()
        to_right(block, j)
        to_left(block, j)
        share(block)
        pick_rows(v, j - 1)
        return 0

    attention_tables(n, v)
    attention_constants(n, v)
    fetch.wait()
    lax.fori_loop(1, n, first_step, 0)
    for t in range(n - 1, v.cache_v.shape[0] // 2):
        pick_rows(v, t)

    def take_right(s, j, forward):
        block = place(-offset_of(j), -s)
        ref = g_ref.at[c, block]
        send(ref, ref, v.right_send, v.right_recv.at[(s - 1) * n + j], partner).wait_recv()
        if forward:
            to_right(block, s * n + j)
        share(block)

    def take_left(s, j, forward):
        block = place(-offset_of(j), s)
        ref = g_ref.at[c, block]
        send(ref, ref, v.left_send, v.left_recv.at[(s - 1) * n + j], partner).wait_recv()
        if forward:
            to_left(block, s * n + j)
        share(block)

    for s in range(1, half + 1):
        if s == half:

            def last_step(j, _):
                take_right(half, j, False)
                take_left(half, j + half, False)
                return 0

            lax.fori_loop(0, half, last_step, 0)
        elif s == half - 1:

            def low_step(j, _):
                take_right(half - 1, j, True)
                take_left(half - 1, j, False)
                return 0

            def high_step(j, _):
                take_right(half - 1, j, False)
                take_left(half - 1, j, True)
                return 0

            lax.fori_loop(0, half, low_step, 0)
            lax.fori_loop(half, n, high_step, 0)
        else:

            def mid_step(j, _, s=s):
                take_right(s, j, True)
                take_left(s, j, True)
                return 0

            lax.fori_loop(0, n, mid_step, 0)

    ring_blocks = n * (half - 1) + half
    some = g_ref.at[c, pl.ds(0, n - 1)]
    send(some, some, v.first_send, v.first_recv.at[0], partner).wait_send()
    some = g_ref.at[c, pl.ds(0, ring_blocks)]
    send(some, some, v.right_send, v.first_recv.at[0], partner).wait_send()
    send(some, some, v.left_send, v.first_recv.at[0], partner).wait_send()
    send(g_ref.at[c], g_ref.at[c], v.share_send, v.share_recv, partner).wait_send()
    send(g_ref.at[1 - c], g_ref.at[1 - c], v.share_send, v.share_recv, partner).wait_recv()


def attend_part(n, latent, v, c):
    heads = n * n
    block_tiles, requests = v.gathered.shape[2], v.gathered.shape[3]
    span, slots = v.pages.shape
    page_rows, width, page_count = v.cache_v.shape
    latent_tiles = latent // LANES
    query_count = v.q.shape[0]
    group = min(requests, heads)
    unroll = min(slots, 4)

    def spread(block, _):
        h = block * group
        for i in range(query_count):
            base = pl.multiple_of(i * heads + h, group)

            def turned(t):
                stack = jnp.concatenate(
                    [v.gathered[t // block_tiles, h + u, t % block_tiles] for u in range(group)], axis=0
                )
                return jnp.dot(v.turn[0], stack, preferred_element_type=f32)

            def keep(t, tile):
                for r in range(requests):
                    v.qr[r, pl.ds(base, group), pl.ds(t * LANES, LANES)] = tile[r * group : (r + 1) * group].astype(bf16)

            for t in range(latent_tiles):
                keep(t, turned(i * latent_tiles + t))
            rotary = turned(query_count * latent_tiles + i // 2)
            keep(latent_tiles, pltpu.roll(rotary, ROPE, 1) if i % 2 else rotary)
        return 0

    lax.fori_loop(0, heads // group, spread, 0)

    def slot_step(g, _):
        held = []
        for u in range(unroll):
            s = g * unroll + u
            r = v.req[s]
            scores = (
                lax.dot_general(
                    v.qr[r, :, :width], v.keys_v[s], (((1,), (1,)), ((), ())), preferred_element_type=f32
                )
                * softmax_scale
            )
            limit = (v.counts[r] - v.start[s]) * page_rows - (query_count - 1)
            visible = (v.place[...] < v.live[s] * page_rows) & (v.shift[...] < limit)
            slot_max = jnp.max(jnp.where(visible, scores, neg_floor), axis=1, keepdims=True)
            weights = jnp.exp(jnp.where(visible, scores - slot_max, neg_floor))
            slot_sum = jnp.sum(weights, axis=1, keepdims=True)
            held.append((weights.astype(bf16), slot_max, slot_sum))
        for u in range(unroll):
            s = g * unroll + u
            p = v.before[s]
            weights, slot_max, slot_sum = held[u]
            old = v.mrep[p]
            new = jnp.maximum(old, slot_max)
            kept = jnp.exp(old - new)
            added = jnp.exp(slot_max - new)
            v.mrep[s] = new
            v.lrep[s] = v.lrep[p] * kept + added * slot_sum
            for t in range(0, latent_tiles, 2):
                out = jnp.dot(weights, v.keys_v[s, :, t * LANES : (t + 2) * LANES], preferred_element_type=f32)
                for w in range(2):
                    v.acc[s, t + w] = v.acc[p, t + w] * kept + out[:, w * LANES : (w + 1) * LANES] * added
        return 0

    lax.fori_loop(0, slots // unroll, slot_step, 0)
    last = [v.last[r] for r in range(requests)]
    head_lane = lax.broadcasted_iota(jnp.int32, (heads, LANES), 1)
    stats = jnp.zeros((heads, LANES), f32)
    for i in range(query_count):
        for r in range(requests):
            at = pl.ds(i * heads, heads)
            stats = jnp.where(head_lane == i * requests + r, v.mrep[last[r], at, :], stats)
            stats = jnp.where(head_lane == (query_count + i) * requests + r, v.lrep[last[r], at, :], stats)
    v.flat[...] = stats
    for a in range(n):
        v.stat[0, a] = v.flat[pl.ds(a * n, n), :]
        v.stat[1, a] = v.flat[pl.ds(a, n, stride=n), :]


def put_side(n, latent, v, side):
    heads = n * n
    requests = v.counts.shape[0]
    query_count = v.q.shape[0]
    group = min(requests, heads)
    side_tiles = latent // LANES // 2
    last = [v.last[r] for r in range(requests)]

    def put(block, _):
        h = block * group
        for i in range(query_count):
            base = pl.multiple_of(i * heads + h, group)
            for t in range(side_tiles):
                tile = side * side_tiles + t
                stack = jnp.concatenate(
                    [v.acc[last[r], tile, pl.ds(base, group), :] for r in range(requests)], axis=0
                )
                flat = jnp.dot(v.turn[1], stack.astype(bf16), preferred_element_type=f32).astype(bf16)
                for u in range(group):
                    high, low = (h + u) // n, (h + u) % n
                    a = high * (1 - side) + low * side
                    b = low * (1 - side) + high * side
                    v.part[side, a, b, i, :, pl.ds(t * LANES, LANES)] = flat[u * requests : (u + 1) * requests]
        return 0

    lax.fori_loop(0, heads // group, put, 0)


def combine_part(n, v, x, y, c, first_peer, second_peer, partner):
    a_here = x * (1 - c) + y * c
    b_here = y * (1 - c) + x * c
    _h, query_count, requests, cols = v.chip_part.shape[1:]
    m_lanes = query_count * requests
    order = list(range(n - 1, -1, -1))

    def a_at(d):
        return (a_here + d + n) % n

    def b_at(d):
        return (b_here + d + n) % n

    stat_swap = send(v.stat.at[1 - c], v.pair_stat, v.sem_pair_stat.at[0], v.sem_pair_stat.at[1], partner)
    stat_swap.start()
    put_side(n, 2 * cols, v, 1 - c)
    for j in order:
        a_pair = (b_here + offset_of(j) + n) % n
        send(
            v.part.at[1 - c, a_pair], v.pair_part.at[a_pair], v.sem_pair_part.at[0, j], v.sem_pair_part.at[1, j], partner
        ).start()
    put_side(n, 2 * cols, v, c)
    stat_swap.wait()

    lane8 = lax.broadcasted_iota(jnp.int32, (n, LANES), 1)
    lane16 = lax.broadcasted_iota(jnp.int32, (requests, LANES), 1)
    row16 = lax.broadcasted_iota(jnp.int32, (requests, LANES), 0)

    def column(row, base):
        picked = jnp.where(lane16 == row16 + base, jnp.broadcast_to(row, (requests, LANES)), 0.0)
        return jnp.sum(picked, axis=1, keepdims=True)

    def merged(all_stats):
        best = all_stats[0]
        for one in all_stats[1:]:
            best = jnp.maximum(best, one)
        factors = [jnp.exp(one - best) for one in all_stats]
        denom = 0.0
        for factor, one in zip(factors, all_stats):
            denom = denom + pltpu.roll(factor, m_lanes, 1) * one
        return factors, jnp.where(lane8 < m_lanes, best, denom)

    for a in range(n):
        factors, stats = merged([v.stat[c, a], v.pair_stat[a]])
        v.f_mine[a] = factors[0]
        v.f_pair[a] = factors[1]
        v.chip_stat[a] = stats
    for j in order[:-1]:
        send(
            v.chip_stat.at[a_at(offset_of(j))], v.ring_stat.at[j], v.sem_stat_a.at[0, j], v.sem_stat_a.at[1, j],
            first_peer(offset_of(j)),
        ).start()
    v.ring_stat[0] = v.chip_stat[a_here]

    def pair_chunk(j, _):
        a_pair = (b_here + offset_of(j) + n) % n
        a = a_at(offset_of(j))
        send(
            v.part.at[1 - c, a_pair], v.pair_part.at[a], v.sem_pair_part.at[0, j], v.sem_pair_part.at[1, j], partner
        ).wait()
        f_m = v.f_mine[a]
        f_p = v.f_pair[a]
        for b in range(n):
            for i in range(query_count):
                mine = v.part[c, a, b, i].astype(f32) * column(f_m[b : b + 1], i * requests)
                theirs = v.pair_part[a, b, i].astype(f32) * column(f_p[b : b + 1], i * requests)
                v.chip_part[a, b, i] = (mine + theirs).astype(bf16)
        return a

    for j in order:
        a = pair_chunk(j, 0)
        if j:
            send(
                v.chip_part.at[a], v.ring_part.at[j], v.sem_part_a.at[0, j], v.sem_part_a.at[1, j], first_peer(offset_of(j))
            ).start()

    for j in range(1, n):
        send(
            v.chip_stat.at[a_here], v.ring_stat.at[j], v.sem_stat_a.at[0, j], v.sem_stat_a.at[1, j], first_peer(offset_of(j))
        ).wait()
    factors, stats = merged([v.ring_stat[j] for j in range(n)])
    for j in range(n):
        v.f_ring[j] = factors[j]
    v.col_stat_send[...] = stats
    for j in order[:-1]:
        send(
            v.col_stat_send, v.col_stat.at[j], v.sem_stat_b.at[0, j], v.sem_stat_b.at[1, j], second_peer(offset_of(j))
        ).start()
    v.col_stat[0] = stats
    for j in range(1, n):
        send(
            v.col_stat_send, v.col_stat.at[j], v.sem_stat_b.at[0, j], v.sem_stat_b.at[1, j], second_peer(offset_of(j))
        ).wait()
    factors, stats = merged([v.col_stat[j] for j in range(n)])
    for j in range(n):
        v.f_col[j] = factors[j]
    v.f_col[n] = stats
    lse = stats + jnp.log(pltpu.roll(jnp.where(lane8 < m_lanes, 1.0, stats), LANES - m_lanes, 1))
    v.lse_send[...] = lse
    v.lse_all[a_here] = lse
    for j in range(1, n):
        send(
            v.lse_send, v.lse_all.at[a_here], v.sem_lse.at[0, j], v.sem_lse.at[1, j], first_peer(offset_of(j))
        ).start()

    for j in range(n):
        if j:
            send(
                v.chip_part.at[a_here], v.ring_part.at[j], v.sem_part_a.at[0, j], v.sem_part_a.at[1, j],
                first_peer(offset_of(j)),
            ).wait()
        factor = v.f_ring[j]
        for b in range(n):
            for i in range(query_count):
                scale = column(factor[b : b + 1], i * requests)
                if j == 0:
                    v.total[b, i] = v.chip_part[a_here, b, i].astype(f32) * scale
                elif j < n - 1:
                    v.total[b, i] = v.total[b, i] + v.ring_part[j, b, i].astype(f32) * scale
                else:
                    v.col_send_part[b, i] = (v.total[b, i] + v.ring_part[j, b, i].astype(f32) * scale).astype(bf16)
    for j in order[:-1]:
        send(
            v.col_send_part.at[b_at(offset_of(j))], v.col_part.at[j], v.sem_part_b.at[0, j], v.sem_part_b.at[1, j],
            second_peer(offset_of(j)),
        ).start()
    sums = [0.0] * query_count
    for j in range(n):
        if j:
            send(
                v.col_send_part.at[b_here], v.col_part.at[j], v.sem_part_b.at[0, j], v.sem_part_b.at[1, j],
                second_peer(offset_of(j)),
            ).wait()
        row = v.f_col[j, pl.ds(b_here, 1), :]
        for i in range(query_count):
            block = v.col_send_part[b_here, i] if j == 0 else v.col_part[j, i]
            sums[i] = sums[i] + block.astype(f32) * column(row, i * requests)
    row = v.f_col[n, pl.ds(b_here, 1), :]
    for i in range(query_count):
        v.out[i] = (sums[i] / column(row, m_lanes + i * requests)).astype(bf16)
    for j in range(1, n):
        a_from = a_at(-offset_of(j))
        send(
            v.lse_send, v.lse_all.at[a_from], v.sem_lse.at[0, j], v.sem_lse.at[1, j], first_peer(offset_of(j))
        ).wait()
    heads = n * n
    for a in range(n):
        v.flat[pl.ds(a * n, n), :] = v.lse_all[a]
    turned = jnp.concatenate([v.flat[pl.ds(a, n, stride=n), :] for a in range(n)], axis=0)
    lse = jnp.where(c == 0, v.flat[...], turned)
    if heads < LANES:
        lse = jnp.concatenate([lse, jnp.zeros((LANES - heads, LANES), f32)], axis=0)
    lse = jnp.transpose(lse)
    for i in range(query_count):
        v.lse[i] = lse[i * requests : (i + 1) * requests, :heads]


def decode(q, cache, pages, tables, n, latent):
    query_count, requests, _held = q.shape
    page_rows, width, page_count = cache.shape
    span, slots = pages.shape
    heads = n * n
    rows = heads * query_count
    cols = latent // 2
    tiles = latent // LANES
    block_tiles = (query_count * tiles + 2) // 2
    size = requests * min(requests, heads)
    dma = pltpu.SemaphoreType.DMA
    vmem = pl.BlockSpec(memory_space=pltpu.VMEM)
    smem = pl.BlockSpec(memory_space=pltpu.SMEM)
    block = (n, n, query_count, requests, cols)
    one = (n, query_count, requests, cols)
    scratch = dict(
        cache_v=pltpu.VMEM(cache.shape, bf16),
        cache_sem=dma,
        gathered=pltpu.VMEM((2, heads, block_tiles, requests, LANES), bf16),
        other=pltpu.VMEM(q.shape, bf16),
        before=pltpu.SMEM((slots,), jnp.int32),
        last=pltpu.SMEM((requests,), jnp.int32),
        pair_send=dma, pair_recv=dma, first_send=dma, first_recv=dma((n,)), right_send=dma,
        right_recv=dma((n * n // 2,)), left_send=dma, left_recv=dma((n * n // 2,)), share_send=dma, share_recv=dma,
        sel=pltpu.VMEM((slots * span, page_count), bf16),
        keys_v=pltpu.VMEM((slots, page_rows * span, width), bf16),
        qr=pltpu.VMEM((requests, rows, (tiles + 1) * LANES), bf16),
        acc=pltpu.VMEM((slots + 1, tiles, rows, LANES), f32),
        mrep=pltpu.VMEM((slots + 1, rows, LANES), f32),
        lrep=pltpu.VMEM((slots + 1, rows, LANES), f32),
        turn=pltpu.VMEM((2, size, size), bf16),
        place=pltpu.VMEM((rows, LANES), jnp.int32),
        shift=pltpu.VMEM((rows, LANES), jnp.int32),
        flat=pltpu.VMEM((heads, LANES), f32),
        part=pltpu.VMEM((2,) + block, bf16),
        stat=pltpu.VMEM((2, n, n, LANES), f32),
        pair_part=pltpu.VMEM(block, bf16),
        pair_stat=pltpu.VMEM((n, n, LANES), f32),
        f_mine=pltpu.VMEM((n, n, LANES), f32),
        f_pair=pltpu.VMEM((n, n, LANES), f32),
        chip_part=pltpu.VMEM(block, bf16),
        chip_stat=pltpu.VMEM((n, n, LANES), f32),
        ring_part=pltpu.VMEM(block, bf16),
        ring_stat=pltpu.VMEM((n, n, LANES), f32),
        f_ring=pltpu.VMEM((n, n, LANES), f32),
        total=pltpu.VMEM(one, f32),
        col_send_part=pltpu.VMEM(one, bf16),
        col_stat_send=pltpu.VMEM((n, LANES), f32),
        col_part=pltpu.VMEM(one, bf16),
        col_stat=pltpu.VMEM((n, n, LANES), f32),
        f_col=pltpu.VMEM((n + 1, n, LANES), f32),
        lse_send=pltpu.VMEM((n, LANES), f32),
        lse_all=pltpu.VMEM((n, n, LANES), f32),
        sem_pair_stat=dma((2,)),
        sem_pair_part=dma((2, n)), sem_stat_a=dma((2, n)), sem_part_a=dma((2, n)), sem_stat_b=dma((2, n)),
        sem_part_b=dma((2, n)), sem_lse=dma((2, n)),
    )
    names = ["q", "cache", "pages", "req", "start", "live", "counts", "out", "lse"] + list(scratch)
    return pl.pallas_call(
        functools.partial(decode_kernel, n, latent, names),
        out_shape=(
            jax.ShapeDtypeStruct((query_count, requests, cols), bf16),
            jax.ShapeDtypeStruct((query_count, requests, heads), f32),
        ),
        in_specs=[vmem, pl.BlockSpec(memory_space=pl.ANY), vmem] + [smem] * 4,
        out_specs=(vmem, vmem),
        scratch_shapes=list(scratch.values()),
        compiler_params=pltpu.CompilerParams(
            collective_id=0, has_side_effects=True, vmem_limit_bytes=62 * 2**20
        ),
        name="decode",
    )(q, cache, pages, *tables)


def per_device(n, queries, cache, page_counts, slot_request, slot_start, slot_live, slot_pages):
    latent = cache.shape[2] - ROPE
    tables = (slot_request, slot_start, slot_live, page_counts)
    out, lse = decode(
        jnp.transpose(queries, (1, 0, 2)), jnp.transpose(cache, (1, 2, 0)), slot_pages.T, tables, n, latent
    )
    return jnp.transpose(out, (1, 0, 2)), jnp.transpose(lse, (1, 0, 2))


def solution(mesh):
    n = round((mesh.shape["kv"] // 2) ** 0.5)
    split = Mesh(mesh.devices.reshape(mesh.shape["rep"], n, n, 2), REP_KV)
    placed = (
        P("rep", None, KV),
        P(REP_KV, None, None),
        P("rep"),
        P(REP_KV),
        P(REP_KV),
        P(REP_KV),
        P(REP_KV, None),
    )
    return jax.shard_map(
        functools.partial(per_device, n),
        mesh=split,
        in_specs=placed,
        out_specs=(P("rep", None, KV), P("rep", None, None)),
        check_vma=False,
    )
```

time: 131 us -> 92.4 us (0.71)
  Pallas kernels: 124 us -> 87.8 us
  other arithmetic: 2.4 us -> 0 us
    pallas_call x3 -> x1, Pallas kernels: 124 us -> 87.8 us  [decode(): pl.pallas_call(functools.partial(decode_kernel, n, latent, names), out_sh...]
    select_n x1 -> x0, other arithmetic: 1.55 us -> none  [per_device(): q = jnp.where(core == 0, low, high)]
    unnamed x1 -> x2, local copies, waits for them, and re-layouts: 1.35 us -> 2.69 us
where the time goes in v2:
time: 92.4 us; the launch traced here: 91.2 us
  Pallas kernels  87.8 us (95%)
  local copies, waits for them, and re-layouts  2.69 us (3%)
    pallas_call x1, Pallas kernels, decode(): pl.pallas_call(functools.partial(decode_kernel, n, latent, names), out_sh...  87.8 us
    unnamed x2, local copies, waits for them, and re-layouts  2.69 us

profile of v2, /device:TPU:514, one launch (start us, length us, event | category | flops | bytes accessed | tf_op | source)
XLA Modules:
  0.0 91.2 jit_solution(13330967843425436771)
XLA Ops:
  0.6 87.8 %decode.1 = (bf16[3,16,256]{2,1,0:T(8,128)(2,1)}, f32[3,16,64]{2,1,0:T(8,128)}) custom-call(bf16[3,16,288]{2,1,0:T(8,128)(2,1)} %bitcast.6, bf16[16,576,256]{2,1,0:T(8,128)(2,1)} %bitcast.5, s32[8,32]{1,0:T(8,128)} %bitcast.9, s32[32]{0:T(128)} %refs_3_.1, s32[32]{0:T(128)} %refs_4_.1, s32[32]{0:T(128)} %refs_5_.1, s32[16]{0:T(128)} %refs_6_.1), custom_call_target="tpu_custom_call" | custom-call | tf_op jit(solution)/shard_map/decode/pallas_call | solution.py:583
  88.5 1.3 %copy.11 = bf16[16,3,256]{2,0,1:T(8,128)(2,1)} copy(bf16[16,3,256]{2,0,1:T(8,128)(2,1)} %bitcast.8) | data formatting | bytes 49152
  89.8 1.3 %copy.12 = f32[16,3,64]{2,0,1:T(8,128)} copy(f32[16,3,64]{2,0,1:T(8,128)} %bitcast.7) | data formatting | bytes 24576

commit v3 on v2

--- a/solution.py
+++ b/solution.py
@@ -62,6 +62,7 @@
     gather_part(n, v, x, y, c, first_peer, second_peer, partner, fetch)
     attend_part(n, latent, v, c)
     combine_part(n, v, x, y, c, first_peer, second_peer, partner)
+    gather_sent(n, v, c, partner)
 
 
 def attention_tables(n, v):
@@ -131,6 +132,7 @@
     g_ref, q_ref, other = v.gathered, v.q, v.other
     swap = send(q_ref, other, v.pair_send, v.pair_recv, partner)
     swap.start()
+    attention_constants(n, v)
     swap.wait()
 
     def place(a, b):
@@ -188,15 +190,12 @@
         to_right(block, j)
         to_left(block, j)
         share(block)
-        pick_rows(v, j - 1)
         return 0
 
     attention_tables(n, v)
-    attention_constants(n, v)
+    lax.fori_loop(1, n, first_step, 0)
     fetch.wait()
-    lax.fori_loop(1, n, first_step, 0)
-    for t in range(n - 1, v.cache_v.shape[0] // 2):
-        pick_rows(v, t)
+    pairs = v.cache_v.shape[0] // 2
 
     def take_right(s, j, forward):
         block = place(-offset_of(j), -s)
@@ -242,18 +241,27 @@
             def mid_step(j, _, s=s):
                 take_right(s, j, True)
                 take_left(s, j, True)
+                if s == 1 and n == pairs:
+                    pick_rows(v, j)
                 return 0
 
             lax.fori_loop(0, n, mid_step, 0)
 
+    if n != pairs or half < 3:
+        for t in range(pairs):
+            pick_rows(v, t)
+    send(g_ref.at[1 - c], g_ref.at[1 - c], v.share_send, v.share_recv, partner).wait_recv()
+
+
+def gather_sent(n, v, c, partner):
+    half = n // 2
     ring_blocks = n * (half - 1) + half
-    some = g_ref.at[c, pl.ds(0, n - 1)]
+    some = v.gathered.at[c, pl.ds(0, n - 1)]
     send(some, some, v.first_send, v.first_recv.at[0], partner).wait_send()
-    some = g_ref.at[c, pl.ds(0, ring_blocks)]
+    some = v.gathered.at[c, pl.ds(0, ring_blocks)]
     send(some, some, v.right_send, v.first_recv.at[0], partner).wait_send()
     send(some, some, v.left_send, v.first_recv.at[0], partner).wait_send()
-    send(g_ref.at[c], g_ref.at[c], v.share_send, v.share_recv, partner).wait_send()
-    send(g_ref.at[1 - c], g_ref.at[1 - c], v.share_send, v.share_recv, partner).wait_recv()
+    send(v.gathered.at[c], v.gathered.at[c], v.share_send, v.share_recv, partner).wait_send()
 
 
 def attend_part(n, latent, v, c):
@@ -418,8 +426,14 @@
             first_peer(offset_of(j)),
         ).start()
     v.ring_stat[0] = v.chip_stat[a_here]
-
-    def pair_chunk(j, _):
+    half = n // 2
+    signs = (1, -1)
+    row8 = lax.broadcasted_iota(jnp.int32, (n, LANES), 0)
+    far = row8 < 0
+    for j in range(half, n):
+        far = far | (row8 == b_at(offset_of(j)))
+
+    def pair_chunk(j):
         a_pair = (b_here + offset_of(j) + n) % n
         a = a_at(offset_of(j))
         send(
@@ -432,65 +446,155 @@
                 mine = v.part[c, a, b, i].astype(f32) * column(f_m[b : b + 1], i * requests)
                 theirs = v.pair_part[a, b, i].astype(f32) * column(f_p[b : b + 1], i * requests)
                 v.chip_part[a, b, i] = (mine + theirs).astype(bf16)
-        return a
-
-    for j in order:
-        a = pair_chunk(j, 0)
-        if j:
+
+    def chain_block(side, step, j, src):
+        return send(
+            src, v.chain_in.at[side, step - 1, b_at(offset_of(j))], v.sem_chain.at[0, side, step - 1, j],
+            v.sem_chain.at[1, side, step - 1, j], first_peer(signs[side]),
+        )
+
+    def chain_best(side, step):
+        return send(
+            v.best_out.at[side, step - 1], v.best_in.at[side, step - 1], v.sem_best.at[0, side, step - 1],
+            v.sem_best.at[1, side, step - 1], first_peer(signs[side]),
+        )
+
+    def chain_first():
+        a = a_at(half)
+        for side in range(2):
+            mine = far if side == 0 else ~far
+            v.best_out[side, 0] = jnp.where(mine, v.chip_stat[a], neg_floor)
+            chain_best(side, 1).start()
+
+        def both(k, _):
+            for side in range(2):
+                j = (n - 1 if side == 0 else half - 1) - k
+                chain_block(side, 1, j, v.chip_part.at[a, b_at(offset_of(j))]).start()
+            return 0
+
+        lax.fori_loop(0, half, both, 0)
+
+    def chain_join(side, step, j, a):
+        chain_block(side, step - 1, j, v.chip_part.at[0, 0]).wait_recv()
+        b = b_at(offset_of(j))
+        f_in = v.f_chain[side, 0, pl.ds(b, 1), :]
+        f_own = v.f_chain[side, 1, pl.ds(b, 1), :]
+        for i in range(query_count):
+            came = v.chain_in[side, step - 2, b, i].astype(f32) * column(f_in, i * requests)
+            mine = v.chip_part[a, b, i].astype(f32) * column(f_own, i * requests)
+            v.chain_out[side, step - 2, b, i] = (came + mine).astype(bf16)
+        chain_block(side, step, j, v.chain_out.at[side, step - 2, b]).start()
+
+    def chain_step(step):
+        targets = [a_at(signs[side] * (half + 1 - step)) for side in range(2)]
+        if step == 2:
+
+            def alone(k, _):
+                for side in range(2):
+                    j = (half - 1 if side == 0 else n - 1) - k
+                    chain_block(side, 2, j, v.chip_part.at[targets[side], b_at(offset_of(j))]).start()
+                return 0
+
+            lax.fori_loop(0, half, alone, 0)
+        for side in range(2):
+            chain_best(side, step - 1).wait_recv()
+            came = v.best_in[side, step - 2]
+            mine = v.chip_stat[targets[side]]
+            best = jnp.maximum(came, mine)
+            v.f_chain[side, 0] = jnp.exp(came - best)
+            v.f_chain[side, 1] = jnp.exp(mine - best)
+            v.best_out[side, step - 1] = best
+            chain_best(side, step).start()
+        if step == 2:
+
+            def joined(k, _):
+                for side in range(2):
+                    chain_join(side, 2, (n - 1 if side == 0 else half - 1) - k, targets[side])
+                return 0
+
+            lax.fori_loop(0, half, joined, 0)
+        else:
+
+            def joined(k, _):
+                for side in range(2):
+                    chain_join(side, step, n - 1 - k, targets[side])
+                return 0
+
+            lax.fori_loop(0, n, joined, 0)
+
+    def ring_stats():
+        for j in range(1, n):
             send(
-                v.chip_part.at[a], v.ring_part.at[j], v.sem_part_a.at[0, j], v.sem_part_a.at[1, j], first_peer(offset_of(j))
-            ).start()
-
-    for j in range(1, n):
-        send(
-            v.chip_stat.at[a_here], v.ring_stat.at[j], v.sem_stat_a.at[0, j], v.sem_stat_a.at[1, j], first_peer(offset_of(j))
-        ).wait()
-    factors, stats = merged([v.ring_stat[j] for j in range(n)])
-    for j in range(n):
-        v.f_ring[j] = factors[j]
-    v.col_stat_send[...] = stats
-    for j in order[:-1]:
-        send(
-            v.col_stat_send, v.col_stat.at[j], v.sem_stat_b.at[0, j], v.sem_stat_b.at[1, j], second_peer(offset_of(j))
-        ).start()
-    v.col_stat[0] = stats
-    for j in range(1, n):
-        send(
-            v.col_stat_send, v.col_stat.at[j], v.sem_stat_b.at[0, j], v.sem_stat_b.at[1, j], second_peer(offset_of(j))
-        ).wait()
-    factors, stats = merged([v.col_stat[j] for j in range(n)])
-    for j in range(n):
-        v.f_col[j] = factors[j]
-    v.f_col[n] = stats
-    lse = stats + jnp.log(pltpu.roll(jnp.where(lane8 < m_lanes, 1.0, stats), LANES - m_lanes, 1))
-    v.lse_send[...] = lse
-    v.lse_all[a_here] = lse
-    for j in range(1, n):
-        send(
-            v.lse_send, v.lse_all.at[a_here], v.sem_lse.at[0, j], v.sem_lse.at[1, j], first_peer(offset_of(j))
-        ).start()
-
-    for j in range(n):
-        if j:
-            send(
-                v.chip_part.at[a_here], v.ring_part.at[j], v.sem_part_a.at[0, j], v.sem_part_a.at[1, j],
+                v.chip_stat.at[a_here], v.ring_stat.at[j], v.sem_stat_a.at[0, j], v.sem_stat_a.at[1, j],
                 first_peer(offset_of(j)),
             ).wait()
-        factor = v.f_ring[j]
-        for b in range(n):
-            for i in range(query_count):
-                scale = column(factor[b : b + 1], i * requests)
-                if j == 0:
-                    v.total[b, i] = v.chip_part[a_here, b, i].astype(f32) * scale
-                elif j < n - 1:
-                    v.total[b, i] = v.total[b, i] + v.ring_part[j, b, i].astype(f32) * scale
-                else:
-                    v.col_send_part[b, i] = (v.total[b, i] + v.ring_part[j, b, i].astype(f32) * scale).astype(bf16)
-    for j in order[:-1]:
+        _factors, stats = merged([v.ring_stat[j] for j in range(n)])
+        v.col_stat_send[...] = stats
+        for j in order[:-1]:
+            send(
+                v.col_stat_send, v.col_stat.at[j], v.sem_stat_b.at[0, j], v.sem_stat_b.at[1, j],
+                second_peer(offset_of(j)),
+            ).start()
+        v.col_stat[0] = stats
+
+    def column_stats():
+        for j in range(1, n):
+            send(
+                v.col_stat_send, v.col_stat.at[j], v.sem_stat_b.at[0, j], v.sem_stat_b.at[1, j],
+                second_peer(offset_of(j)),
+            ).wait()
+        factors, stats = merged([v.col_stat[j] for j in range(n)])
+        for j in range(n):
+            v.f_col[j] = factors[j]
+        v.f_col[n] = stats
+        lse = stats + jnp.log(pltpu.roll(jnp.where(lane8 < m_lanes, 1.0, stats), LANES - m_lanes, 1))
+        v.lse_send[...] = lse
+        v.lse_all[a_here] = lse
+        for j in range(1, n):
+            send(
+                v.lse_send, v.lse_all.at[a_here], v.sem_lse.at[0, j], v.sem_lse.at[1, j], first_peer(offset_of(j))
+            ).start()
+
+    pair_chunk(n - 1)
+    chain_first()
+    for step in range(2, half + 1):
+        pair_chunk(2 * (half + 1 - step))
+        pair_chunk(2 * (half + 1 - step) - 1)
+        chain_step(step)
+        if step == 2:
+            ring_stats()
+    column_stats()
+    pair_chunk(0)
+    for side in range(2):
+        chain_best(side, half).wait_recv()
+    best = v.col_stat_send[...]
+    v.f_ring[0] = jnp.exp(v.chip_stat[a_here] - best)
+    for side in range(2):
+        v.f_ring[1 + side] = jnp.exp(v.best_in[side, half - 1] - best)
+
+    def finish(j):
+        b = b_at(offset_of(j))
+        rows = [v.f_ring[k, pl.ds(b, 1), :] for k in range(3)]
+        for side in range(2):
+            chain_block(side, half, j, v.chip_part.at[0, 0]).wait_recv()
+        for i in range(query_count):
+            total = v.chip_part[a_here, b, i].astype(f32) * column(rows[0], i * requests)
+            for side in range(2):
+                came = v.chain_in[side, half - 1, b, i].astype(f32)
+                total = total + came * column(rows[1 + side], i * requests)
+            v.col_send_part[b, i] = total.astype(bf16)
+
+    def finish_far(k, _):
+        j = n - 1 - k
+        finish(j)
         send(
             v.col_send_part.at[b_at(offset_of(j))], v.col_part.at[j], v.sem_part_b.at[0, j], v.sem_part_b.at[1, j],
             second_peer(offset_of(j)),
         ).start()
+        return 0
+
+    lax.fori_loop(0, n - 1, finish_far, 0)
+    finish(0)
     sums = [0.0] * query_count
     for j in range(n):
         if j:
@@ -505,6 +609,17 @@
     row = v.f_col[n, pl.ds(b_here, 1), :]
     for i in range(query_count):
         v.out[i] = (sums[i] / column(row, m_lanes + i * requests)).astype(bf16)
+    for side in range(2):
+        for step in range(1, half + 1):
+            chain_best(side, step).wait_send()
+
+            def sent(j, _, side=side, step=step):
+                chain_block(side, step, j, v.chip_part.at[0, 0]).wait_send()
+                return 0
+
+            first = half if (step, side) == (1, 0) else 0
+            end = half if (step, side) == (1, 1) else n
+            lax.fori_loop(first, end, sent, 0)
     for j in range(1, n):
         a_from = a_at(-offset_of(j))
         send(
@@ -564,10 +679,13 @@
         f_pair=pltpu.VMEM((n, n, LANES), f32),
         chip_part=pltpu.VMEM(block, bf16),
         chip_stat=pltpu.VMEM((n, n, LANES), f32),
-        ring_part=pltpu.VMEM(block, bf16),
+        chain_in=pltpu.VMEM((2, n // 2) + one, bf16),
+        chain_out=pltpu.VMEM((2, n // 2) + one, bf16),
+        best_in=pltpu.VMEM((2, n // 2, n, LANES), f32),
+        best_out=pltpu.VMEM((2, n // 2, n, LANES), f32),
+        f_chain=pltpu.VMEM((2, 2, n, LANES), f32),
         ring_stat=pltpu.VMEM((n, n, LANES), f32),
-        f_ring=pltpu.VMEM((n, n, LANES), f32),
-        total=pltpu.VMEM(one, f32),
+        f_ring=pltpu.VMEM((3, n, LANES), f32),
         col_send_part=pltpu.VMEM(one, bf16),
         col_stat_send=pltpu.VMEM((n, LANES), f32),
         col_part=pltpu.VMEM(one, bf16),
@@ -576,7 +694,7 @@
         lse_send=pltpu.VMEM((n, LANES), f32),
         lse_all=pltpu.VMEM((n, n, LANES), f32),
         sem_pair_stat=dma((2,)),
-        sem_pair_part=dma((2, n)), sem_stat_a=dma((2, n)), sem_part_a=dma((2, n)), sem_stat_b=dma((2, n)),
+        sem_pair_part=dma((2, n)), sem_stat_a=dma((2, n)), sem_chain=dma((2, 2, n // 2, n)), sem_best=dma((2, 2, n // 2)), sem_stat_b=dma((2, n)),
         sem_part_b=dma((2, n)), sem_lse=dma((2, n)),
     )
     names = ["q", "cache", "pages", "req", "start", "live", "counts", "out", "lse"] + list(scratch)

time: 92.4 us -> 86.8 us (0.939)
  Pallas kernels: 87.8 us -> 82.8 us
    pallas_call x1, Pallas kernels: 87.8 us -> 82.8 us  [decode(): pl.pallas_call(functools.partial(decode_kernel, n, latent, names), out_sh...]
where the time goes in v3:
time: 86.8 us; the launch traced here: 86.1 us
  Pallas kernels  82.8 us (95%)
  local copies, waits for them, and re-layouts  2.69 us (3%)
    pallas_call x1, Pallas kernels, decode(): pl.pallas_call(functools.partial(decode_kernel, n, latent, names), out_sh...  82.8 us
    unnamed x2, local copies, waits for them, and re-layouts  2.69 us

profile of v3, /device:TPU:514, one launch (start us, length us, event | category | flops | bytes accessed | tf_op | source)
XLA Modules:
  0.0 86.1 jit_solution(11176987278795020694)
XLA Ops:
  0.6 82.8 %decode.1 = (bf16[3,16,256]{2,1,0:T(8,128)(2,1)}, f32[3,16,64]{2,1,0:T(8,128)}) custom-call(bf16[3,16,288]{2,1,0:T(8,128)(2,1)} %bitcast.6, bf16[16,576,256]{2,1,0:T(8,128)(2,1)} %bitcast.5, s32[8,32]{1,0:T(8,128)} %bitcast.9, s32[32]{0:T(128)} %refs_3_.1, s32[32]{0:T(128)} %refs_4_.1, s32[32]{0:T(128)} %refs_5_.1, s32[16]{0:T(128)} %refs_6_.1), custom_call_target="tpu_custom_call" | custom-call | tf_op jit(solution)/shard_map/decode/pallas_call | solution.py:701
  83.4 1.3 %copy.11 = bf16[16,3,256]{2,0,1:T(8,128)(2,1)} copy(bf16[16,3,256]{2,0,1:T(8,128)(2,1)} %bitcast.8) | data formatting | bytes 49152
  84.8 1.3 %copy.12 = f32[16,3,64]{2,0,1:T(8,128)} copy(f32[16,3,64]{2,0,1:T(8,128)} %bitcast.7) | data formatting | bytes 24576
